TPU v7x, 256 devices: a whole 4x4x8 slice. The times are simulated.
256 devices in a mesh: gx: 8 (over x_hi, y), gy: 32 (over z, x_lo, core).
Axes of the slice: x: 4 (x_hi: 2, x_lo: 2; x = x_hi * 2 + x_lo), y: 4, z: 8, core: 2. Of those that a mesh axis runs over, the one named last changes fastest.
Arguments:
- charges: float32 [8, 32, 16384], P('gx', 'gy'), may hold values from -1.2 to 1.2
- fractions: float32 [8, 32, 3, 16384], P('gx', 'gy'), may hold values from 0 to 1
- cells: int32 [8, 32, 2, 16384], P('gx', 'gy'), may hold values from 0 to 511, as said below
Outputs:
- potential_grid: float32 [256, 512, 128], P('gx', 'gy')
- atom_potential: float32 [8, 32, 16384], P('gx', 'gy')
Inputs may be any that keep to these rules, and one draw needn't show every extreme that they name: cells[i, j, 0, a] lies in i-independent range j * 16 + 1 to j * 16 + 16, taken modulo 512; cells[i, j, 1, a] is a cell along the third dimension.
All inputs are finite; a program needn't handle non-finite values.
Results may differ from a plain program's by a relative error of at most 0.0003.
Values sent between devices are 32-bit elements; how exact they have to be, the bound alone decides.
A program may use at most 128 MiB of HBM per device.

v0:
```python
import functools

import jax
import jax.numpy as jnp
import numpy as np
from jax import lax
from jax.experimental import pallas as pl
from jax.experimental.pallas import tpu as pltpu
from jax.sharding import PartitionSpec as P

CX = 32
CY = 16
NZ = 128
ATOMS_DEV = 16384
N_GX = 8
N_GY = 32
PLANE = ATOMS_DEV // CX
EX = CX + 3
EY = 24
MESH_IDS = pl.DeviceIdType.MESH
BF16 = jnp.bfloat16
F32 = jnp.float32
taps = ((-3, -0.0625), (-1, 0.5625), (0, 1.0), (1, 0.5625), (3, -0.0625))


def smooth_numpy(rho):
    return np.where(
        rho < 1.0, 1.875 - 1.25 * rho * rho + 0.375 * rho**4, 1.0 / np.maximum(rho, 1.0)
    )


def frequencies(count):
    inner = np.repeat(np.arange(1, count // 2), 2)
    return np.concatenate([[0], inner, [count // 2]])


def real_basis(count):
    wave = frequencies(count)
    angle = 2.0 * np.pi * wave[:, None] * np.arange(count)[None, :] / count
    is_sine = np.zeros(count, bool)
    is_sine[2:-1:2] = True
    basis = np.where(is_sine[:, None], np.sin(angle), np.cos(angle)) * np.sqrt(2.0 / count)
    basis[0] /= np.sqrt(2.0)
    basis[-1] /= np.sqrt(2.0)
    return basis


def restriction(count):
    matrix = np.zeros((count // 2, count))
    for row in range(count // 2):
        for offset, weight in taps:
            matrix[row, (2 * row + offset) % count] += weight
    return matrix


def stencil_table(level, extent):
    offsets = np.arange(-3, 4) * 1.0
    radius = np.sqrt(
        offsets[:, None, None] ** 2 + offsets[None, :, None] ** 2 + offsets[None, None, :] ** 2
    )
    stencil = (smooth_numpy(radius / 1.5) / 1.5 - smooth_numpy(radius / 3.0) / 3.0) / 2.0 ** (
        level - 1
    )
    waves = np.cos(2.0 * np.pi * offsets[:, None] * frequencies(extent)[None, :] / extent)
    table = np.zeros((16, 128))
    table[:, :extent] = (stencil[3:, 3:] @ waves).reshape(16, extent)
    return table.astype(np.float32)


def placed_at(block, row, column):
    matrix = np.zeros((128, 128))
    matrix[row : row + block.shape[0], column : column + block.shape[1]] = block
    return matrix


(
    C_M12,
    C_M23,
    C_BD0,
    C_BD1,
    C_NZ0,
    C_NZ1,
    C_M23T,
    C_M12T,
    C_UR,
    C_PU,
) = (0, 1, 5, 6, 7, 8, 9, 10, 11, 12)


@functools.cache
def split_constants():
    def down(count):
        return (real_basis(count // 2) @ restriction(count) @ real_basis(count).T).T

    m12, m23, m34 = down(128), down(64), down(32)
    stack = [placed_at(m12, 0, 0)]
    stack += [placed_at(m23, 0, 32 * place) for place in range(4)]
    for half in range(2):
        matrix = np.zeros((128, 128))
        for place in range(4):
            matrix += placed_at(m34, 32 * place, 64 * half + 16 * place)
        stack.append(matrix)
    for half in range(2):
        matrix = np.zeros((128, 128))
        for place in range(4):
            matrix += placed_at(m34.T, 64 * half + 16 * place, 0)
        stack.append(matrix)
    stack += [placed_at(m23.T, 0, 0), placed_at(m12.T, 0, 0)]
    along_x = restriction(64)
    columns = (np.arange(64) - 8) % 64
    stack.append(placed_at((real_basis(32) @ along_x)[:, columns], 0, 0))
    rows = (np.arange(16) - 2) % 64
    stack.append(placed_at((real_basis(32) @ along_x).T[rows], 0, 0))
    return split_pair(np.stack(stack))


def split_pair(matrix):
    high = matrix.astype(np.float32).astype(BF16)
    low = (matrix - high.astype(np.float64)).astype(np.float32).astype(BF16)
    return high, low


@functools.cache
def coarse_table():
    counts = (32, 64, 16)
    signed = [np.where(np.arange(c) > c // 2, np.arange(c) - c, np.arange(c)) for c in counts]
    radius = np.sqrt(
        signed[0][:, None, None] ** 2.0
        + signed[1][None, :, None] ** 2.0
        + signed[2][None, None, :] ** 2.0
    )
    kernel = smooth_numpy(radius / 1.5) / 12.0
    wave_x = np.cos(2.0 * np.pi * np.outer(frequencies(32), np.arange(32)) / 32)
    wave_z = np.cos(2.0 * np.pi * np.outer(frequencies(16), np.arange(16)) / 16)
    along_y = np.einsum("ax,xyz,bz->aby", wave_x, kernel, wave_z)
    down_y = restriction(128)
    differ = (np.arange(64)[:, None] - np.arange(64)[None, :]) % 64
    up_rows = down_y.T[(np.arange(4) - 2) % 128]
    folded = np.einsum("cm,abmn->abcn", up_rows, along_y[:, :, differ])
    folded = np.einsum("abcn,ny->abcy", folded, down_y)
    folded = folded.reshape(2, 16, 16, 4, 32, 4).transpose(3, 4, 1, 0, 5, 2)
    folded = folded.reshape(4, 32, 16, 128)
    extended = folded[:, (np.arange(34) - 2) % 32]
    return extended.astype(np.float32)


def split(value):
    high = value.astype(BF16)
    low = (value - high.astype(F32)).astype(BF16)
    return high, low


def mm(a, b):
    return jnp.dot(a, b, preferred_element_type=F32)


def times_const(value, high_w, low_w):
    high, low = split(value)
    return mm(high, high_w) + (mm(low, high_w) + mm(high, low_w))


def const_times(high_w, low_w, value):
    high, low = split(value)
    return mm(high_w, high) + (mm(high_w, low) + mm(low_w, high))


def spline_weights(frac):
    def near_weight(distance):
        return (1.0 - distance) * (1.0 + distance - 1.5 * distance * distance)

    def far_weight(distance):
        return -0.5 * (distance - 1.0) * (2.0 - distance) * (2.0 - distance)

    return (
        far_weight(1.0 + frac),
        near_weight(frac),
        near_weight(1.0 - frac),
        far_weight(2.0 - frac),
    )


def tap_table(distance, weights):
    result = jnp.zeros(distance.shape, F32)
    for tap in range(4):
        result = jnp.where(distance == tap, weights[tap], result)
    return result


def plane_tables(plane, fraction_ref, cell_ref, index_y):
    lanes = pl.ds(pl.multiple_of(plane * PLANE, PLANE), PLANE)
    weights = spline_weights(fraction_ref[:, lanes])
    cells = cell_ref[:, lanes]
    base_y = (cells[0:1] - (index_y * CY + 1)) & (CY * N_GY - 1)
    base_z = cells[1:2] - 1
    places_y = lax.broadcasted_iota(jnp.int32, (EY, PLANE), 0)
    places_z = lax.broadcasted_iota(jnp.int32, (NZ, PLANE), 0)
    table_y = tap_table(places_y - base_y, [w[1:2] for w in weights])
    table_z = tap_table((places_z - base_z) & (NZ - 1), [w[2:3] for w in weights])
    return lanes, [w[0:1] for w in weights], table_y, table_z


def deposit_kernel(charge_ref, fraction_ref, cell_ref, high_ref, low_ref, grid_ref, edge_ref, sums):
    index_y = lax.axis_index("gy")
    sums[...] = jnp.zeros_like(sums)

    def step(plane, carried):
        lanes, along_x, table_y, table_z = plane_tables(plane, fraction_ref, cell_ref, index_y)
        charge = charge_ref[:, lanes]
        spread = jnp.concatenate([table_y * (w * charge) for w in along_x], axis=0)
        spread_high, spread_low = split(spread)
        z_high, z_low = split(table_z)
        dims = (((1,), (1,)), ((), ()))
        both = jnp.concatenate([spread_high, spread_low], axis=0)
        first = lax.dot_general(both, z_high, dims, preferred_element_type=F32)
        second = lax.dot_general(spread_high, z_low, dims, preferred_element_type=F32)
        contrib = first[: 4 * EY] + first[4 * EY :] + second
        for tap in range(4):
            sums[plane + tap] = sums[plane + tap] + contrib[EY * tap : EY * (tap + 1)]
        return carried

    lax.fori_loop(0, CX, step, 0)
    flat = sums[...].reshape(EX * EY, NZ)
    grid_ref[...] = times_const(flat, high_ref[...], low_ref[...]).reshape(EX, EY, NZ)
    edge_ref[...] = grid_ref[:, 11:19, :]


def sample_kernel(
    field_ref, fraction_ref, cell_ref, high_ref, low_ref, grid_ref, atom_ref, window_ref
):
    index_y = lax.axis_index("gy")
    flat = field_ref[...].reshape(EX * EY, NZ)
    window_ref[...] = times_const(flat, high_ref[...], low_ref[...]).reshape(EX, EY, NZ)
    grid_ref[...] = window_ref[:CX, :CY, :]

    def step(plane, carried):
        lanes, along_x, table_y, table_z = plane_tables(plane, fraction_ref, cell_ref, index_y)
        window = window_ref[pl.ds(plane, 4)].reshape(4 * EY, NZ)
        high, low = split(window)
        z_high, z_low = split(table_z)
        projected = mm(
            jnp.concatenate([high, low], axis=1), jnp.concatenate([z_high, z_high], axis=0)
        ) + mm(high, z_low)
        total = jnp.zeros((EY, PLANE), F32)
        for tap in range(4):
            total = total + along_x[tap] * projected[EY * tap : EY * (tap + 1)]
        atom_ref[:, lanes] = jnp.sum(total * table_y, axis=0, keepdims=True)
        return carried

    lax.fori_loop(0, CX, step, 0)


NEIGHBOURS = ((1, 0), (-1, 0), (0, 1), (0, -1), (1, 1), (1, -1), (-1, 1), (-1, -1))
N_SEMS = 8 + 8 + 7 + 4 + 31


def prolonged_rows(get, row):
    middle = row // 2
    if row % 2 == 0:
        return get(middle)
    return 0.5625 * (get(middle) + get(middle + 1)) - 0.0625 * (get(middle - 1) + get(middle + 2))


def levels_kernel(
    own_ref,
    edge_ref,
    k1_ref,
    k2_ref,
    k3_ref,
    high_ref,
    low_ref,
    table_hbm,
    out_ref,
    from_x,
    from_y,
    from_corner,
    q1,
    sums1,
    smooth1,
    part1,
    q2,
    smooth2,
    part2,
    ring_x,
    halo,
    ring_y,
    q3,
    field3,
    up3,
    up2,
    table,
    table_sem,
    send_sems,
    recv_sems,
):
    index_x = lax.axis_index("gx")
    index_y = lax.axis_index("gy")

    def device(step_x, step_y):
        return (
            lax.rem(index_x + (step_x + N_GX), N_GX),
            lax.rem(index_y + (step_y + N_GY), N_GY),
        )

    table_copy = pltpu.make_async_copy(table_hbm, table, table_sem)
    table_copy.start()

    barrier = pltpu.get_barrier_semaphore()
    peers = [(x, 0) for x in range(1, N_GX)] + [(0, y) for y in range(1, N_GY)]
    peers += [(x, y) for x, y in NEIGHBOURS if x and y]
    for step_x, step_y in peers:
        pl.semaphore_signal(
            barrier, inc=1, device_id=device(step_x, step_y), device_id_type=MESH_IDS
        )
    pl.semaphore_wait(barrier, len(peers))

    started = []

    def send(number, source, target, step_x, step_y):
        copy = pltpu.make_async_remote_copy(
            src_ref=source,
            dst_ref=target,
            send_sem=send_sems.at[number],
            recv_sem=recv_sems.at[number],
            device_id=device(step_x, step_y),
            device_id_type=MESH_IDS,
        )
        copy.start()
        started.append(copy)
        return copy

    low_x, high_x = pl.ds(0, 6), pl.ds(29, 6)
    round1 = [
        send(0, own_ref.at[high_x], from_x.at[0], 1, 0),
        send(1, own_ref.at[low_x], from_x.at[1], -1, 0),
        send(2, edge_ref, from_y.at[0], 0, 1),
        send(3, own_ref.at[:, 0:8, :], from_y.at[1], 0, -1),
        send(4, edge_ref.at[high_x], from_corner.at[0], 1, 1),
        send(5, own_ref.at[high_x, 0:8, :], from_corner.at[1], 1, -1),
        send(6, edge_ref.at[low_x], from_corner.at[2], -1, 1),
        send(7, own_ref.at[low_x, 0:8, :], from_corner.at[3], -1, -1),
    ]

    zero_tile = jnp.zeros((8, NZ), F32)

    def clear(x, carried):
        q1[x, 0:8, :] = zero_tile
        q1[x, 32:40, :] = zero_tile
        return carried

    lax.fori_loop(0, 41, clear, 0)
    for x in (0, 1, 2, 38, 39, 40):
        q1[x, 8:32, :] = jnp.zeros((EY, NZ), F32)

    def copy_own(x, carried):
        q1[x + 3, 8:32, :] = own_ref[x]
        return carried

    lax.fori_loop(0, EX, copy_own, 0)
    q2[:, 24:32, :] = jnp.zeros((26, 8, NZ), F32)
    q3[:, 24:32, :] = jnp.zeros((15, 8, NZ), F32)

    for copy in round1:
        copy.wait_recv()

    def add_y(x, carried):
        q1[x + 3, 3:11, :] = q1[x + 3, 3:11, :] + from_y[0, x]
        q1[x + 3, 24:32, :] = q1[x + 3, 24:32, :] + from_y[1, x]
        return carried

    lax.fori_loop(0, EX, add_y, 0)
    for side, start in ((0, 0), (1, 35)):
        for x in range(6):
            row = start + x
            q1[row, 8:32, :] = q1[row, 8:32, :] + from_x[side, x]
            q1[row, 3:11, :] = q1[row, 3:11, :] + from_corner[2 * side, x]
            q1[row, 24:32, :] = q1[row, 24:32, :] + from_corner[2 * side + 1, x]

    def restrict_y(x, carried):
        total = jnp.zeros((8, NZ), F32)
        for offset, weight in taps:
            total = total + weight * q1[x, pl.ds(8 + offset, 8, stride=2), :]
        part1[x] = total
        return carried

    lax.fori_loop(0, 37, restrict_y, 0)
    rows = []
    for m in range(16):
        total = jnp.zeros((8, NZ), F32)
        for offset, weight in taps:
            total = total + weight * part1[2 * m + 3 + offset]
        rows.append(total)
    level2 = times_const(jnp.concatenate(rows, axis=0), high_ref[C_M12], low_ref[C_M12])
    q2[4:20, 8:16, :] = level2.reshape(16, 8, NZ)

    round2 = []
    for number, (step_x, step_y) in enumerate(NEIGHBOURS):
        source_x, target_x, count = {0: (4, 4, 16), 1: (16, 0, 4), -1: (4, 20, 6)}[step_x]
        target_y = {0: 8, 1: 0, -1: 16}[step_y]
        round2.append(
            send(
                8 + number,
                q2.at[pl.ds(source_x, count), 8:16, :],
                q2.at[pl.ds(target_x, count), pl.ds(target_y, 8), :],
                step_x,
                step_y,
            )
        )

    def sum_y(x, carried):
        for dy in range(1, 4):
            sums1[dy - 1, x] = q1[x, 8 + dy : 32 + dy, :] + q1[x, 8 - dy : 32 - dy, :]
        return carried

    lax.fori_loop(0, 41, sum_y, 0)

    def stencil1(x, carried):
        total = jnp.zeros((EY, NZ), F32)
        for dy in range(4):
            for dx in range(4):
                if dy == 0:
                    value = q1[x + 3 + dx, 8:32, :]
                    if dx:
                        value = value + q1[x + 3 - dx, 8:32, :]
                else:
                    value = sums1[dy - 1, x + 3 + dx]
                    if dx:
                        value = value + sums1[dy - 1, x + 3 - dx]
                total = total + k1_ref[4 * dx + dy : 4 * dx + dy + 1, :] * value
        smooth1[x] = total
        return carried

    lax.fori_loop(0, EX, stencil1, 0)

    for copy in round2:
        copy.wait_recv()

    for m in range(8):
        total = jnp.zeros((24, NZ), F32)
        for offset, weight in taps:
            total = total + weight * q2[2 * m + 4 + offset, 0:24, :]
        part2[24 * m : 24 * (m + 1), :] = total
    tile = jnp.zeros((8, NZ), F32)
    for n in range(4):
        total = jnp.zeros((8, NZ), F32)
        for offset, weight in taps:
            total = total + weight * part2[pl.ds(8 + 2 * n + offset, 8, stride=24), :]
        tile = tile + times_const(total, high_ref[C_M23 + n], low_ref[C_M23 + n])
    ring_x[1] = tile

    round3 = []
    for step in range(1, N_GX):
        place = (N_GX - step + 1) % N_GX
        round3.append(send(15 + step, ring_x.at[1], ring_x.at[place], step, 0))

    def stencil_small(source, row, start, count, k_ref):
        total = jnp.zeros((count, NZ), F32)
        for across in range(4):
            for along in range(4):
                value = None
                for sign_r in sorted({across, -across}):
                    for sign_s in sorted({along, -along}):
                        piece = source[row + sign_r, start + sign_s : start + sign_s + count, :]
                        value = piece if value is None else value + piece
                total = total + k_ref[4 * across + along : 4 * across + along + 1, :] * value
        return total

    def stencil2(x, carried):
        smooth2[x] = stencil_small(q2, x + 3, 7, 16, k2_ref)
        return carried

    lax.fori_loop(0, 20, stencil2, 0)

    for copy in round3:
        copy.wait_recv()

    round4 = []
    for number, step in enumerate((1, -1, 2, -2)):
        round4.append(send(23 + number, ring_x.at[0:3], halo.at[2 - step], 0, step))
    column = const_times(
        high_ref[C_UR, 0:32, 0:64], low_ref[C_UR, 0:32, 0:64], ring_x[...].reshape(64, NZ)
    )
    ring_y[0] = times_const(column[0:16], high_ref[C_BD0], low_ref[C_BD0]) + times_const(
        column[16:32], high_ref[C_BD1], low_ref[C_BD1]
    )
    round5 = []
    for step in range(1, N_GY):
        round5.append(send(26 + step, ring_y.at[0], ring_y.at[N_GY - step], 0, step))

    halo[2] = ring_x[0:3]
    for copy in round4:
        copy.wait_recv()
    for y in range(-5, 10):
        place = y % 4
        source = halo[y // 4 + 2].reshape(24, NZ)
        if place:
            source = pltpu.roll(source, NZ - 32 * place, axis=1)
        q3[y + 5, 0:24, :] = source

    def stencil3(y, carried):
        field3[y] = stencil_small(q3, y + 3, 6, 16, k3_ref)
        return carried

    lax.fori_loop(0, 9, stencil3, 0)

    table_copy.wait()
    for copy in round5:
        copy.wait_recv()
    coarse = []
    for row in range(9):
        kind, shift = row % 4, row // 4

        def add_slot(slot, total, kind=kind, shift=shift):
            return total + table[kind, slot + 2 - shift] * ring_y[slot]

        coarse.append(lax.fori_loop(0, N_GY, add_slot, jnp.zeros((16, NZ), F32), unroll=4))
    coarse = jnp.concatenate(coarse, axis=0)
    half0 = times_const(coarse, high_ref[C_NZ0], low_ref[C_NZ0])
    half1 = times_const(coarse, high_ref[C_NZ1], low_ref[C_NZ1])
    for row in range(9):
        both = jnp.concatenate(
            [half0[16 * row : 16 * (row + 1)], half1[16 * row : 16 * (row + 1)]], axis=0
        )
        field3[row] = field3[row] + const_times(
            high_ref[C_PU, 0:16, 0:32], low_ref[C_PU, 0:16, 0:32], both
        )

    fields = [prolonged_rows(lambda m: field3[m + 2], y) for y in range(-1, 11)]
    up3[...] = times_const(jnp.concatenate(fields, axis=0), high_ref[C_M23T], low_ref[C_M23T])

    def column3(m):
        return up3[pl.ds(m + 2, 12, stride=16), :]

    for x in range(-1, 19):
        smooth2[x + 1, 0:12, :] = smooth2[x + 1, 0:12, :] + prolonged_rows(column3, x)

    part = times_const(
        smooth2[...].reshape(20 * 16, NZ), high_ref[C_M12T], low_ref[C_M12T]
    ).reshape(20, 16, NZ)
    smooth2[...] = part

    def widen_y(x, carried):
        rows = [smooth2[x, n : n + 12, :] for n in range(4)]
        up2[x, pl.ds(0, 12, stride=2), :] = rows[1]
        up2[x, pl.ds(1, 12, stride=2), :] = 0.5625 * (rows[1] + rows[2]) - 0.0625 * (
            rows[0] + rows[3]
        )
        return carried

    lax.fori_loop(0, 20, widen_y, 0)

    def widen_x(m, carried):
        values = [up2[m + n] for n in range(4)]
        out_ref[2 * m] = smooth1[2 * m] + values[1]
        out_ref[2 * m + 1] = smooth1[2 * m + 1] + (
            0.5625 * (values[1] + values[2]) - 0.0625 * (values[0] + values[3])
        )
        return carried

    lax.fori_loop(0, 17, widen_x, 0)
    out_ref[34] = smooth1[34] + up2[18]

    for copy in started:
        copy.wait_send()


def in_vmem(count):
    return [pl.BlockSpec(memory_space=pltpu.VMEM)] * count


def local(charges, fractions, cells):
    charge = charges.reshape(1, ATOMS_DEV)
    fraction = fractions.reshape(3, ATOMS_DEV)
    cell = cells.reshape(2, ATOMS_DEV)
    forward = [jnp.asarray(part) for part in split_pair(real_basis(NZ).T)]
    inverse = [jnp.asarray(part) for part in split_pair(real_basis(NZ))]
    block = jax.ShapeDtypeStruct((EX, EY, NZ), F32)

    own, edge = pl.pallas_call(
        deposit_kernel,
        out_shape=(block, jax.ShapeDtypeStruct((EX, 8, NZ), F32)),
        in_specs=in_vmem(5),
        out_specs=in_vmem(2),
        scratch_shapes=[pltpu.VMEM((EX, EY, NZ), F32)],
        name="deposit",
    )(charge, fraction, cell, *forward)

    high, low = split_constants()
    field = pl.pallas_call(
        levels_kernel,
        out_shape=block,
        in_specs=in_vmem(7) + [pl.BlockSpec(memory_space=pl.ANY)],
        out_specs=pl.BlockSpec(memory_space=pltpu.VMEM),
        scratch_shapes=[
            pltpu.VMEM((2, 6, EY, NZ), F32),
            pltpu.VMEM((2, EX, 8, NZ), F32),
            pltpu.VMEM((4, 6, 8, NZ), F32),
            pltpu.VMEM((41, 40, NZ), F32),
            pltpu.VMEM((3, 41, EY, NZ), F32),
            pltpu.VMEM((EX, EY, NZ), F32),
            pltpu.VMEM((37, 8, NZ), F32),
            pltpu.VMEM((26, 32, NZ), F32),
            pltpu.VMEM((20, 16, NZ), F32),
            pltpu.VMEM((8 * 24, NZ), F32),
            pltpu.VMEM((N_GX, 8, NZ), F32),
            pltpu.VMEM((5, 3, 8, NZ), F32),
            pltpu.VMEM((N_GY, 16, NZ), F32),
            pltpu.VMEM((15, 32, NZ), F32),
            pltpu.VMEM((9, 16, NZ), F32),
            pltpu.VMEM((12 * 16, NZ), F32),
            pltpu.VMEM((20, EY, NZ), F32),
            pltpu.VMEM((4, 34, 16, NZ), F32),
            pltpu.SemaphoreType.DMA,
            pltpu.SemaphoreType.DMA((N_SEMS,)),
            pltpu.SemaphoreType.DMA((N_SEMS,)),
        ],
        compiler_params=pltpu.CompilerParams(collective_id=0, has_side_effects=True),
        name="levels",
    )(
        own,
        edge,
        jnp.asarray(stencil_table(1, 128)),
        jnp.asarray(stencil_table(2, 64)),
        jnp.asarray(stencil_table(3, 32)),
        jnp.asarray(high),
        jnp.asarray(low),
        jnp.asarray(coarse_table()),
    )

    potential, sampled = pl.pallas_call(
        sample_kernel,
        out_shape=(
            jax.ShapeDtypeStruct((CX, CY, NZ), F32),
            jax.ShapeDtypeStruct((1, ATOMS_DEV), F32),
        ),
        in_specs=in_vmem(5),
        out_specs=in_vmem(2),
        scratch_shapes=[pltpu.VMEM((EX, EY, NZ), F32)],
        name="sample",
    )(field, fraction, cell, *inverse)
    return potential, sampled.reshape(1, 1, ATOMS_DEV)


def solution(mesh):
    placed = (P("gx", "gy", None), P("gx", "gy", None, None), P("gx", "gy", None, None))
    return jax.shard_map(
        local,
        mesh=mesh,
        in_specs=placed,
        out_specs=(P("gx", "gy", None), P("gx", "gy", None)),
        check_vma=False,
    )
```

profile of v0, /device:TPU:1, one launch (start us, length us, event | category | flops | bytes accessed | tf_op | source)
XLA Modules:
  0.0 73.3 jit_solution(3016463645520861173)
XLA Ops:
  0.6 1.8 %copy.17 = f32[1,1,3,16384]{3,2,1,0:T(4,128)} copy(f32[1,1,3,16384]{3,1,2,0:T(1,128)} %param.14) | data formatting | bytes 393216
  2.4 13.5 %deposit.1 = (f32[35,24,128]{2,1,0:T(8,128)}, f32[35,8,128]{2,1,0:T(8,128)}) custom-call(f32[1,16384]{1,0:T(1,128)} %bitcast.10, f32[3,16384]{1,0:T(4,128)} %bitcast.6, s32[2,16384]{1,0:T(2,128)} %bitcast.8, bf16[128,128]{1,0:T(8,128)(2,1)} %constant.20.clone.high_ref, bf16[128,128]{1,0:T(8,128)(2,1)} %constant.21.clone.low_ref), custom_call_target="tpu_custom_call" | custom-call | tf_op jit(solution)/shard_map/deposit/pallas_call | solution.py:578
  15.9 44.4 %levels.1.field_ref = f32[35,24,128]{2,1,0:T(8,128)} custom-call(f32[35,24,128]{2,1,0:T(8,128)} %get-tuple-element.6.own_ref, f32[35,8,128]{2,1,0:T(8,128)} %get-tuple-element.7.edge_ref, f32[16,128]{1,0:T(8,128)} %constant.24.clone.k1_ref, f32[16,128]{1,0:T(8,128)} %constant.25.clone.k2_ref, f32[16,128]{1,0:T(8,128)} %constant.26.clone.k3_ref, ...), custom_call_target="tpu_custom_call" | custom-call | tf_op jit(solution)/shard_map/levels/pallas_call | solution.py:588
  60.3 13.0 %sample.1 = (f32[32,16,128]{2,1,0:T(8,128)}, f32[1,16384]{1,0:T(1,128)}) custom-call(f32[35,24,128]{2,1,0:T(8,128)} %levels.1.field_ref, f32[3,16384]{1,0:T(4,128)} %bitcast.7, s32[2,16384]{1,0:T(2,128)} %bitcast.9, bf16[128,128]{1,0:T(8,128)(2,1)} %constant.22.clone.high_ref, bf16[128,128]{1,0:T(8,128)(2,1)} %constant.23.clone.low_ref), custom_call_target="tpu_custom_call" | custom-call | tf_op jit(solution)/shard_map/sample/pallas_call | solution.py:629
where the time goes:
time: 73.5 us; the launch traced here: 73.3 us
  Pallas kernels  70.9 us (96%)
  local copies, waits for them, and re-layouts  1.75 us (2%)
    pallas_call x1, Pallas kernels, local(): pl.pallas_call(levels_kernel, out_shape=block, in_specs=in_vmem(7) + [pl....  44.4 us
    pallas_call x1, Pallas kernels, local(): pl.pallas_call(deposit_kernel, out_shape=(block, jax.ShapeDtypeStruct((EX...  13.5 us
    pallas_call x1, Pallas kernels, local(): pl.pallas_call(sample_kernel, out_shape=(jax.ShapeDtypeStruct((CX, CY, NZ...  13 us
    unnamed x1, local copies, waits for them, and re-layouts  1.75 us

commit v1 on v0

--- a/solution.py
+++ b/solution.py
@@ -186,46 +186,61 @@
     return result
 
 
-def plane_tables(plane, fraction_ref, cell_ref, index_y):
+def rows_of(row):
+    packed = jnp.broadcast_to(row, (16, row.shape[1])).astype(BF16)
+    return jnp.concatenate([packed] * (NZ // 16), axis=0)
+
+
+def depth_tables(places_ref, base, weights):
+    places = jnp.concatenate([places_ref[...]] * (base.shape[1] // 128), axis=1)
+    high = low = jnp.zeros(places.shape, BF16)
+    for tap in range(4):
+        target = ((base + tap) & (NZ - 1)).astype(F32)
+        here = places == rows_of(target)
+        weight_high = weights[tap].astype(BF16).astype(F32)
+        high = jnp.where(here, rows_of(weight_high), high)
+        low = jnp.where(here, rows_of(weights[tap] - weight_high), low)
+    return high, low
+
+
+def plane_tables(plane, fraction_ref, cell_ref, places_ref, index_y):
     lanes = pl.ds(pl.multiple_of(plane * PLANE, PLANE), PLANE)
-    weights = spline_weights(fraction_ref[:, lanes])
+    fraction = jnp.concatenate([fraction_ref[k, :, lanes] for k in range(3)], axis=0)
+    weights = spline_weights(fraction)
     cells = cell_ref[:, lanes]
     base_y = (cells[0:1] - (index_y * CY + 1)) & (CY * N_GY - 1)
-    base_z = cells[1:2] - 1
     places_y = lax.broadcasted_iota(jnp.int32, (EY, PLANE), 0)
-    places_z = lax.broadcasted_iota(jnp.int32, (NZ, PLANE), 0)
     table_y = tap_table(places_y - base_y, [w[1:2] for w in weights])
-    table_z = tap_table((places_z - base_z) & (NZ - 1), [w[2:3] for w in weights])
-    return lanes, [w[0:1] for w in weights], table_y, table_z
-
-
-def deposit_kernel(charge_ref, fraction_ref, cell_ref, high_ref, low_ref, grid_ref, edge_ref, sums):
-    index_y = lax.axis_index("gy")
-    sums[...] = jnp.zeros_like(sums)
-
-    def step(plane, carried):
-        lanes, along_x, table_y, table_z = plane_tables(plane, fraction_ref, cell_ref, index_y)
-        charge = charge_ref[:, lanes]
-        spread = jnp.concatenate([table_y * (w * charge) for w in along_x], axis=0)
-        spread_high, spread_low = split(spread)
-        z_high, z_low = split(table_z)
-        dims = (((1,), (1,)), ((), ()))
-        both = jnp.concatenate([spread_high, spread_low], axis=0)
-        first = lax.dot_general(both, z_high, dims, preferred_element_type=F32)
-        second = lax.dot_general(spread_high, z_low, dims, preferred_element_type=F32)
-        contrib = first[: 4 * EY] + first[4 * EY :] + second
-        for tap in range(4):
-            sums[plane + tap] = sums[plane + tap] + contrib[EY * tap : EY * (tap + 1)]
-        return carried
-
-    lax.fori_loop(0, CX, step, 0)
-    flat = sums[...].reshape(EX * EY, NZ)
-    grid_ref[...] = times_const(flat, high_ref[...], low_ref[...]).reshape(EX, EY, NZ)
-    edge_ref[...] = grid_ref[:, 11:19, :]
+    tables_z = depth_tables(places_ref, cells[1:2] - 1, [w[2:3] for w in weights])
+    return lanes, [w[0:1] for w in weights], table_y, tables_z
+
+
+def deposit_plane(plane, charge_ref, fraction_ref, cell_ref, places_ref, sums, index_y):
+    lanes, along_x, table_y, (z_high, z_low) = plane_tables(
+        plane, fraction_ref, cell_ref, places_ref, index_y
+    )
+    charge = charge_ref[:, lanes]
+    spread = jnp.concatenate([table_y * (w * charge) for w in along_x], axis=0)
+    spread_high, spread_low = split(spread)
+    dims = (((1,), (1,)), ((), ()))
+    both = jnp.concatenate([spread_high, spread_low], axis=0)
+    first = lax.dot_general(both, z_high, dims, preferred_element_type=F32)
+    second = lax.dot_general(spread_high, z_low, dims, preferred_element_type=F32)
+    contrib = first[: 4 * EY] + first[4 * EY :] + second
+    for tap in range(4):
+        sums[plane + tap] = sums[plane + tap] + contrib[EY * tap : EY * (tap + 1)]
 
 
 def sample_kernel(
-    field_ref, fraction_ref, cell_ref, high_ref, low_ref, grid_ref, atom_ref, window_ref
+    field_ref,
+    fraction_ref,
+    cell_ref,
+    places_ref,
+    high_ref,
+    low_ref,
+    grid_ref,
+    atom_ref,
+    window_ref,
 ):
     index_y = lax.axis_index("gy")
     flat = field_ref[...].reshape(EX * EY, NZ)
@@ -233,10 +248,11 @@
     grid_ref[...] = window_ref[:CX, :CY, :]
 
     def step(plane, carried):
-        lanes, along_x, table_y, table_z = plane_tables(plane, fraction_ref, cell_ref, index_y)
+        lanes, along_x, table_y, (z_high, z_low) = plane_tables(
+            plane, fraction_ref, cell_ref, places_ref, index_y
+        )
         window = window_ref[pl.ds(plane, 4)].reshape(4 * EY, NZ)
         high, low = split(window)
-        z_high, z_low = split(table_z)
         projected = mm(
             jnp.concatenate([high, low], axis=1), jnp.concatenate([z_high, z_high], axis=0)
         ) + mm(high, z_low)
@@ -246,11 +262,11 @@
         atom_ref[:, lanes] = jnp.sum(total * table_y, axis=0, keepdims=True)
         return carried
 
-    lax.fori_loop(0, CX, step, 0)
+    lax.fori_loop(0, CX, step, 0, unroll=2)
 
 
 NEIGHBOURS = ((1, 0), (-1, 0), (0, 1), (0, -1), (1, 1), (1, -1), (-1, 1), (-1, -1))
-N_SEMS = 8 + 8 + 7 + 4 + 31
+N_SEMS = 16 + 8 + 7 + 4 + 31
 
 
 def prolonged_rows(get, row):
@@ -261,8 +277,12 @@
 
 
 def levels_kernel(
-    own_ref,
-    edge_ref,
+    charge_ref,
+    fraction_ref,
+    cell_ref,
+    places_ref,
+    forward_high_ref,
+    forward_low_ref,
     k1_ref,
     k2_ref,
     k3_ref,
@@ -270,6 +290,9 @@
     low_ref,
     table_hbm,
     out_ref,
+    sums,
+    own,
+    edge,
     from_x,
     from_y,
     from_corner,
@@ -311,7 +334,6 @@
         pl.semaphore_signal(
             barrier, inc=1, device_id=device(step_x, step_y), device_id_type=MESH_IDS
         )
-    pl.semaphore_wait(barrier, len(peers))
 
     started = []
 
@@ -328,17 +350,47 @@
         started.append(copy)
         return copy
 
-    low_x, high_x = pl.ds(0, 6), pl.ds(29, 6)
-    round1 = [
-        send(0, own_ref.at[high_x], from_x.at[0], 1, 0),
-        send(1, own_ref.at[low_x], from_x.at[1], -1, 0),
-        send(2, edge_ref, from_y.at[0], 0, 1),
-        send(3, own_ref.at[:, 0:8, :], from_y.at[1], 0, -1),
-        send(4, edge_ref.at[high_x], from_corner.at[0], 1, 1),
-        send(5, own_ref.at[high_x, 0:8, :], from_corner.at[1], 1, -1),
-        send(6, edge_ref.at[low_x], from_corner.at[2], -1, 1),
-        send(7, own_ref.at[low_x, 0:8, :], from_corner.at[3], -1, -1),
-    ]
+    sums[...] = jnp.zeros_like(sums)
+
+    def deposit(first, last, row, count):
+        def step(plane, carried):
+            deposit_plane(
+                plane, charge_ref, fraction_ref, cell_ref, places_ref, sums, index_y
+            )
+            return carried
+
+        lax.fori_loop(first, last, step, 0, unroll=2)
+        flat = sums[row : row + count].reshape(count * EY, NZ)
+        value = times_const(flat, forward_high_ref[...], forward_low_ref[...])
+        own[row : row + count] = value.reshape(count, EY, NZ)
+        edge[row : row + count] = own[row : row + count, 11:19, :]
+
+    round1 = []
+
+    def send_edges(number, row, count):
+        rows = pl.ds(row, count)
+        round1.append(send(number, edge.at[rows], from_y.at[0, rows], 0, 1))
+        round1.append(send(number + 1, own.at[rows, 0:8, :], from_y.at[1, rows], 0, -1))
+
+    deposit(26, 32, 29, 6)
+    pl.semaphore_wait(barrier, len(peers))
+    high_x = pl.ds(29, 6)
+    round1.append(send(0, edge.at[high_x], from_corner.at[0], 1, 1))
+    round1.append(send(1, own.at[high_x, 0:8, :], from_corner.at[1], 1, -1))
+    round1.append(send(2, own.at[high_x], from_x.at[0], 1, 0))
+    send_edges(6, 29, 6)
+    deposit(0, 6, 0, 6)
+    low_x = pl.ds(0, 6)
+    round1.append(send(3, edge.at[low_x], from_corner.at[2], -1, 1))
+    round1.append(send(4, own.at[low_x, 0:8, :], from_corner.at[3], -1, -1))
+    round1.append(send(5, own.at[low_x], from_x.at[1], -1, 0))
+    send_edges(8, 0, 6)
+    deposit(6, 14, 6, 8)
+    send_edges(10, 6, 8)
+    deposit(14, 22, 14, 8)
+    send_edges(12, 14, 8)
+    deposit(22, 26, 22, 7)
+    send_edges(14, 22, 7)
 
     zero_tile = jnp.zeros((8, NZ), F32)
 
@@ -352,7 +404,7 @@
         q1[x, 8:32, :] = jnp.zeros((EY, NZ), F32)
 
     def copy_own(x, carried):
-        q1[x + 3, 8:32, :] = own_ref[x]
+        q1[x + 3, 8:32, :] = own[x]
         return carried
 
     lax.fori_loop(0, EX, copy_own, 0)
@@ -398,7 +450,7 @@
         target_y = {0: 8, 1: 0, -1: 16}[step_y]
         round2.append(
             send(
-                8 + number,
+                16 + number,
                 q2.at[pl.ds(source_x, count), 8:16, :],
                 q2.at[pl.ds(target_x, count), pl.ds(target_y, 8), :],
                 step_x,
@@ -450,7 +502,7 @@
     round3 = []
     for step in range(1, N_GX):
         place = (N_GX - step + 1) % N_GX
-        round3.append(send(15 + step, ring_x.at[1], ring_x.at[place], step, 0))
+        round3.append(send(23 + step, ring_x.at[1], ring_x.at[place], step, 0))
 
     def stencil_small(source, row, start, count, k_ref):
         total = jnp.zeros((count, NZ), F32)
@@ -475,7 +527,7 @@
 
     round4 = []
     for number, step in enumerate((1, -1, 2, -2)):
-        round4.append(send(23 + number, ring_x.at[0:3], halo.at[2 - step], 0, step))
+        round4.append(send(31 + number, ring_x.at[0:3], halo.at[2 - step], 0, step))
     column = const_times(
         high_ref[C_UR, 0:32, 0:64], low_ref[C_UR, 0:32, 0:64], ring_x[...].reshape(64, NZ)
     )
@@ -484,7 +536,7 @@
     )
     round5 = []
     for step in range(1, N_GY):
-        round5.append(send(26 + step, ring_y.at[0], ring_y.at[N_GY - step], 0, step))
+        round5.append(send(34 + step, ring_y.at[0], ring_y.at[N_GY - step], 0, step))
 
     halo[2] = ring_x[0:3]
     for copy in round4:
@@ -569,28 +621,23 @@
 
 def local(charges, fractions, cells):
     charge = charges.reshape(1, ATOMS_DEV)
-    fraction = fractions.reshape(3, ATOMS_DEV)
+    fraction = fractions.reshape(3, 1, ATOMS_DEV)
     cell = cells.reshape(2, ATOMS_DEV)
+    places = jnp.asarray(np.tile(np.arange(NZ)[:, None], (1, 128)).astype(BF16))
     forward = [jnp.asarray(part) for part in split_pair(real_basis(NZ).T)]
     inverse = [jnp.asarray(part) for part in split_pair(real_basis(NZ))]
     block = jax.ShapeDtypeStruct((EX, EY, NZ), F32)
-
-    own, edge = pl.pallas_call(
-        deposit_kernel,
-        out_shape=(block, jax.ShapeDtypeStruct((EX, 8, NZ), F32)),
-        in_specs=in_vmem(5),
-        out_specs=in_vmem(2),
-        scratch_shapes=[pltpu.VMEM((EX, EY, NZ), F32)],
-        name="deposit",
-    )(charge, fraction, cell, *forward)
 
     high, low = split_constants()
     field = pl.pallas_call(
         levels_kernel,
         out_shape=block,
-        in_specs=in_vmem(7) + [pl.BlockSpec(memory_space=pl.ANY)],
+        in_specs=in_vmem(11) + [pl.BlockSpec(memory_space=pl.ANY)],
         out_specs=pl.BlockSpec(memory_space=pltpu.VMEM),
         scratch_shapes=[
+            pltpu.VMEM((EX, EY, NZ), F32),
+            pltpu.VMEM((EX, EY, NZ), F32),
+            pltpu.VMEM((EX, 8, NZ), F32),
             pltpu.VMEM((2, 6, EY, NZ), F32),
             pltpu.VMEM((2, EX, 8, NZ), F32),
             pltpu.VMEM((4, 6, 8, NZ), F32),
@@ -616,8 +663,11 @@
         compiler_params=pltpu.CompilerParams(collective_id=0, has_side_effects=True),
         name="levels",
     )(
-        own,
-        edge,
+        charge,
+        fraction,
+        cell,
+        places,
+        *forward,
         jnp.asarray(stencil_table(1, 128)),
         jnp.asarray(stencil_table(2, 64)),
         jnp.asarray(stencil_table(3, 32)),
@@ -632,11 +682,11 @@
             jax.ShapeDtypeStruct((CX, CY, NZ), F32),
             jax.ShapeDtypeStruct((1, ATOMS_DEV), F32),
         ),
-        in_specs=in_vmem(5),
+        in_specs=in_vmem(6),
         out_specs=in_vmem(2),
         scratch_shapes=[pltpu.VMEM((EX, EY, NZ), F32)],
         name="sample",
-    )(field, fraction, cell, *inverse)
+    )(field, fraction, cell, places, *inverse)
     return potential, sampled.reshape(1, 1, ATOMS_DEV)
 
 

time: 73.5 us -> 56.2 us (0.76)
  Pallas kernels: 70.9 us -> 55.4 us
  local copies, waits for them, and re-layouts: 1.75 us -> 0 us
    pallas_call x2 -> x1, Pallas kernels: 57.9 us -> 46.6 us  [local(): pl.pallas_call(levels_kernel, out_shape=block, in_specs=in_vmem(11) + [pl...]
    pallas_call x1, Pallas kernels: 13 us -> 8.82 us  [local(): pl.pallas_call(sample_kernel, out_shape=(jax.ShapeDtypeStruct((CX, CY, NZ...]
    unnamed x1 -> x0, local copies, waits for them, and re-layouts: 1.75 us -> none
where the time goes in v1:
time: 56.2 us; the launch traced here: 56 us
  Pallas kernels  55.4 us (99%)
  between operations  0.64 us (1%)
    pallas_call x1, Pallas kernels, local(): pl.pallas_call(levels_kernel, out_shape=block, in_specs=in_vmem(11) + [pl...  46.6 us
    pallas_call x1, Pallas kernels, local(): pl.pallas_call(sample_kernel, out_shape=(jax.ShapeDtypeStruct((CX, CY, NZ...  8.82 us

profile of v1, /device:TPU:1, one launch (start us, length us, event | category | flops | bytes accessed | tf_op | source)
XLA Modules:
  0.0 56.0 jit_solution(7194886499283401783)
XLA Ops:
  0.6 46.6 %levels.1.field_ref = f32[35,24,128]{2,1,0:T(8,128)} custom-call(f32[1,16384]{1,0:T(1,128)} %bitcast.8, f32[3,1,16384]{2,1,0:T(1,128)} %bitcast.4, s32[2,16384]{1,0:T(2,128)} %bitcast.6, bf16[128,128]{1,0:T(8,128)(2,1)} %constant.22.clone.places_ref, bf16[128,128]{1,0:T(8,128)(2,1)} %constant.23.clone.forward_high_ref, ...), custom_call_target="tpu_custom_call" | custom-call | tf_op jit(solution)/shard_map/levels/pallas_call | solution.py:632
  47.2 8.8 %sample.1 = (f32[32,16,128]{2,1,0:T(8,128)}, f32[1,16384]{1,0:T(1,128)}) custom-call(f32[35,24,128]{2,1,0:T(8,128)} %levels.1.field_ref, f32[3,1,16384]{2,1,0:T(1,128)} %bitcast.5, s32[2,16384]{1,0:T(2,128)} %bitcast.7, bf16[128,128]{1,0:T(8,128)(2,1)} %constant.22.clone.places_ref, bf16[128,128]{1,0:T(8,128)(2,1)} %constant.25.clone.high_ref, ...), custom_call_target="tpu_custom_call" | custom-call | tf_op jit(solution)/shard_map/sample/pallas_call | solution.py:679

commit v2 on v1

--- a/solution.py
+++ b/solution.py
@@ -84,7 +84,8 @@
     C_M12T,
     C_UR,
     C_PU,
-) = (0, 1, 5, 6, 7, 8, 9, 10, 11, 12)
+    C_M12B,
+) = (0, 1, 5, 6, 7, 8, 9, 10, 11, 12, 13)
 
 
 @functools.cache
@@ -111,6 +112,7 @@
     stack.append(placed_at((real_basis(32) @ along_x)[:, columns], 0, 0))
     rows = (np.arange(16) - 2) % 64
     stack.append(placed_at((real_basis(32) @ along_x).T[rows], 0, 0))
+    stack.append(placed_at(m12, 0, 64))
     return split_pair(np.stack(stack))
 
 
@@ -296,6 +298,11 @@
     from_x,
     from_y,
     from_corner,
+    from_x2,
+    from_y2,
+    from_corner2,
+    own2,
+    edge2,
     q1,
     sums1,
     smooth1,
@@ -352,7 +359,13 @@
 
     sums[...] = jnp.zeros_like(sums)
 
-    def deposit(first, last, row, count):
+    def clear(x, carried):
+        q1[x] = jnp.zeros((40, NZ), F32)
+        return carried
+
+    lax.fori_loop(0, 41, clear, 0)
+
+    def deposit(first, last, row, count, send_finished):
         def step(plane, carried):
             deposit_plane(
                 plane, charge_ref, fraction_ref, cell_ref, places_ref, sums, index_y
@@ -365,6 +378,17 @@
         own[row : row + count] = value.reshape(count, EY, NZ)
         edge[row : row + count] = own[row : row + count, 11:19, :]
 
+        def restrict_y(x, carried):
+            q1[x + 3, 8:32, :] = own[x]
+            total = jnp.zeros((16, NZ), F32)
+            for offset, weight in taps:
+                total = total + weight * q1[x + 3, pl.ds(6 + offset, 16, stride=2), :]
+            part1[x] = total
+            return carried
+
+        send_finished()
+        lax.fori_loop(row, row + count, restrict_y, 0)
+
     round1 = []
 
     def send_edges(number, row, count):
@@ -372,44 +396,128 @@
         round1.append(send(number, edge.at[rows], from_y.at[0, rows], 0, 1))
         round1.append(send(number + 1, own.at[rows, 0:8, :], from_y.at[1, rows], 0, -1))
 
-    deposit(26, 32, 29, 6)
-    pl.semaphore_wait(barrier, len(peers))
-    high_x = pl.ds(29, 6)
-    round1.append(send(0, edge.at[high_x], from_corner.at[0], 1, 1))
-    round1.append(send(1, own.at[high_x, 0:8, :], from_corner.at[1], 1, -1))
-    round1.append(send(2, own.at[high_x], from_x.at[0], 1, 0))
-    send_edges(6, 29, 6)
-    deposit(0, 6, 0, 6)
-    low_x = pl.ds(0, 6)
-    round1.append(send(3, edge.at[low_x], from_corner.at[2], -1, 1))
-    round1.append(send(4, own.at[low_x, 0:8, :], from_corner.at[3], -1, -1))
-    round1.append(send(5, own.at[low_x], from_x.at[1], -1, 0))
-    send_edges(8, 0, 6)
-    deposit(6, 14, 6, 8)
-    send_edges(10, 6, 8)
-    deposit(14, 22, 14, 8)
-    send_edges(12, 14, 8)
-    deposit(22, 26, 22, 7)
-    send_edges(14, 22, 7)
-
-    zero_tile = jnp.zeros((8, NZ), F32)
-
-    def clear(x, carried):
-        q1[x, 0:8, :] = zero_tile
-        q1[x, 32:40, :] = zero_tile
-        return carried
-
-    lax.fori_loop(0, 41, clear, 0)
-    for x in (0, 1, 2, 38, 39, 40):
-        q1[x, 8:32, :] = jnp.zeros((EY, NZ), F32)
-
-    def copy_own(x, carried):
-        q1[x + 3, 8:32, :] = own[x]
-        return carried
-
-    lax.fori_loop(0, EX, copy_own, 0)
-    q2[:, 24:32, :] = jnp.zeros((26, 8, NZ), F32)
+    high_x, low_x = pl.ds(29, 6), pl.ds(0, 6)
+
+    def send_high():
+        pl.semaphore_wait(barrier, len(peers))
+        round1.append(send(0, edge.at[high_x], from_corner.at[0], 1, 1))
+        round1.append(send(1, own.at[high_x, 0:8, :], from_corner.at[1], 1, -1))
+        round1.append(send(2, own.at[high_x], from_x.at[0], 1, 0))
+        send_edges(6, 29, 6)
+
+    def send_low():
+        round1.append(send(3, edge.at[low_x], from_corner.at[2], -1, 1))
+        round1.append(send(4, own.at[low_x, 0:8, :], from_corner.at[3], -1, -1))
+        round1.append(send(5, own.at[low_x], from_x.at[1], -1, 0))
+        send_edges(8, 0, 6)
+
+    deposit(26, 32, 29, 6, send_high)
+    deposit(0, 6, 0, 6, send_low)
+    deposit(6, 14, 6, 8, lambda: send_edges(10, 6, 8))
+    deposit(14, 22, 14, 8, lambda: send_edges(12, 14, 8))
+    deposit(22, 26, 22, 7, lambda: send_edges(14, 22, 7))
+
+    rows = []
+    for m in range(-1, 19):
+        total = jnp.zeros((16, NZ), F32)
+        for offset, weight in taps:
+            if 0 <= 2 * m + offset < EX:
+                total = total + weight * part1[2 * m + offset]
+        rows.append(total)
+    level2 = times_const(
+        jnp.concatenate(rows[0::2], axis=0), high_ref[C_M12], low_ref[C_M12]
+    ) + times_const(jnp.concatenate(rows[1::2], axis=0), high_ref[C_M12B], low_ref[C_M12B])
+    own2[...] = level2.reshape(10, 16, NZ)
+    edge2[...] = own2[:, 5:13, :]
+
+    round2 = []
+    for number, (step_x, step_y) in enumerate(NEIGHBOURS):
+        rows = {0: pl.ds(0, 10), 1: pl.ds(6, 4), -1: pl.ds(0, 4)}[step_x]
+        if step_y == 0:
+            source, target = own2.at[rows], from_x2.at[number]
+        elif step_x == 0:
+            source = edge2 if step_y == 1 else own2.at[:, 0:8, :]
+            target = from_y2.at[number - 2]
+        else:
+            source = edge2.at[rows] if step_y == 1 else own2.at[rows, 0:8, :]
+            target = from_corner2.at[number - 4]
+        round2.append(send(16 + number, source, target, step_x, step_y))
+
+    q2[...] = jnp.zeros_like(q2)
     q3[:, 24:32, :] = jnp.zeros((15, 8, NZ), F32)
+    for pair in range(10):
+        q2[3 + 2 * pair, 7:23, :] = own2[pair]
+        q2[4 + 2 * pair, 7:23, :] = pltpu.roll(own2[pair], 64, axis=1)
+
+    for copy in round2:
+        copy.wait_recv()
+
+    def add_to2(row, start, value):
+        end = start + value.shape[0]
+        for place, plane in ((row, value), (row + 1, pltpu.roll(value, 64, axis=1))):
+            if 0 <= place < 26:
+                q2[place, start:end, :] = q2[place, start:end, :] + plane
+
+    for pair in range(10):
+        add_to2(3 + 2 * pair, 4, from_y2[0, pair])
+        add_to2(3 + 2 * pair, 15, from_y2[1, pair])
+    for side, first in ((0, -1), (1, 19)):
+        for pair in range(4):
+            add_to2(first + 2 * pair, 7, from_x2[side, pair])
+            add_to2(first + 2 * pair, 4, from_corner2[2 * side, pair])
+            add_to2(first + 2 * pair, 15, from_corner2[2 * side + 1, pair])
+
+    for m in range(8):
+        total = jnp.zeros((24, NZ), F32)
+        for offset, weight in taps:
+            total = total + weight * q2[2 * m + 4 + offset, 0:24, :]
+        part2[24 * m : 24 * (m + 1), :] = total
+    tile = jnp.zeros((8, NZ), F32)
+    for n in range(4):
+        total = jnp.zeros((8, NZ), F32)
+        for offset, weight in taps:
+            total = total + weight * part2[pl.ds(8 + 2 * n + offset, 8, stride=24), :]
+        tile = tile + times_const(total, high_ref[C_M23 + n], low_ref[C_M23 + n])
+    ring_x[1] = tile
+
+    round3 = []
+    for step in range(1, N_GX):
+        place = (N_GX - step + 1) % N_GX
+        round3.append(send(23 + step, ring_x.at[1], ring_x.at[place], step, 0))
+
+    def stencil_small(source, row, start, count, k_ref):
+        total = jnp.zeros((count, NZ), F32)
+        for across in range(4):
+            for along in range(4):
+                value = None
+                for sign_r in sorted({across, -across}):
+                    for sign_s in sorted({along, -along}):
+                        piece = source[row + sign_r, start + sign_s : start + sign_s + count, :]
+                        value = piece if value is None else value + piece
+                total = total + k_ref[4 * across + along : 4 * across + along + 1, :] * value
+        return total
+
+    def stencil2(x, carried):
+        smooth2[x] = stencil_small(q2, x + 3, 7, 16, k2_ref)
+        return carried
+
+    lax.fori_loop(0, 20, stencil2, 0)
+
+    for copy in round3:
+        copy.wait_recv()
+
+    round4 = []
+    for number, step in enumerate((1, -1, 2, -2)):
+        round4.append(send(31 + number, ring_x.at[0:3], halo.at[2 - step], 0, step))
+    column = const_times(
+        high_ref[C_UR, 0:32, 0:64], low_ref[C_UR, 0:32, 0:64], ring_x[...].reshape(64, NZ)
+    )
+    ring_y[0] = times_const(column[0:16], high_ref[C_BD0], low_ref[C_BD0]) + times_const(
+        column[16:32], high_ref[C_BD1], low_ref[C_BD1]
+    )
+    round5 = []
+    for step in range(1, N_GY):
+        round5.append(send(34 + step, ring_y.at[0], ring_y.at[N_GY - step], 0, step))
 
     for copy in round1:
         copy.wait_recv()
@@ -426,37 +534,6 @@
             q1[row, 8:32, :] = q1[row, 8:32, :] + from_x[side, x]
             q1[row, 3:11, :] = q1[row, 3:11, :] + from_corner[2 * side, x]
             q1[row, 24:32, :] = q1[row, 24:32, :] + from_corner[2 * side + 1, x]
-
-    def restrict_y(x, carried):
-        total = jnp.zeros((8, NZ), F32)
-        for offset, weight in taps:
-            total = total + weight * q1[x, pl.ds(8 + offset, 8, stride=2), :]
-        part1[x] = total
-        return carried
-
-    lax.fori_loop(0, 37, restrict_y, 0)
-    rows = []
-    for m in range(16):
-        total = jnp.zeros((8, NZ), F32)
-        for offset, weight in taps:
-            total = total + weight * part1[2 * m + 3 + offset]
-        rows.append(total)
-    level2 = times_const(jnp.concatenate(rows, axis=0), high_ref[C_M12], low_ref[C_M12])
-    q2[4:20, 8:16, :] = level2.reshape(16, 8, NZ)
-
-    round2 = []
-    for number, (step_x, step_y) in enumerate(NEIGHBOURS):
-        source_x, target_x, count = {0: (4, 4, 16), 1: (16, 0, 4), -1: (4, 20, 6)}[step_x]
-        target_y = {0: 8, 1: 0, -1: 16}[step_y]
-        round2.append(
-            send(
-                16 + number,
-                q2.at[pl.ds(source_x, count), 8:16, :],
-                q2.at[pl.ds(target_x, count), pl.ds(target_y, 8), :],
-                step_x,
-                step_y,
-            )
-        )
 
     def sum_y(x, carried):
         for dy in range(1, 4):
@@ -483,61 +560,6 @@
 
     lax.fori_loop(0, EX, stencil1, 0)
 
-    for copy in round2:
-        copy.wait_recv()
-
-    for m in range(8):
-        total = jnp.zeros((24, NZ), F32)
-        for offset, weight in taps:
-            total = total + weight * q2[2 * m + 4 + offset, 0:24, :]
-        part2[24 * m : 24 * (m + 1), :] = total
-    tile = jnp.zeros((8, NZ), F32)
-    for n in range(4):
-        total = jnp.zeros((8, NZ), F32)
-        for offset, weight in taps:
-            total = total + weight * part2[pl.ds(8 + 2 * n + offset, 8, stride=24), :]
-        tile = tile + times_const(total, high_ref[C_M23 + n], low_ref[C_M23 + n])
-    ring_x[1] = tile
-
-    round3 = []
-    for step in range(1, N_GX):
-        place = (N_GX - step + 1) % N_GX
-        round3.append(send(23 + step, ring_x.at[1], ring_x.at[place], step, 0))
-
-    def stencil_small(source, row, start, count, k_ref):
-        total = jnp.zeros((count, NZ), F32)
-        for across in range(4):
-            for along in range(4):
-                value = None
-                for sign_r in sorted({across, -across}):
-                    for sign_s in sorted({along, -along}):
-                        piece = source[row + sign_r, start + sign_s : start + sign_s + count, :]
-                        value = piece if value is None else value + piece
-                total = total + k_ref[4 * across + along : 4 * across + along + 1, :] * value
-        return total
-
-    def stencil2(x, carried):
-        smooth2[x] = stencil_small(q2, x + 3, 7, 16, k2_ref)
-        return carried
-
-    lax.fori_loop(0, 20, stencil2, 0)
-
-    for copy in round3:
-        copy.wait_recv()
-
-    round4 = []
-    for number, step in enumerate((1, -1, 2, -2)):
-        round4.append(send(31 + number, ring_x.at[0:3], halo.at[2 - step], 0, step))
-    column = const_times(
-        high_ref[C_UR, 0:32, 0:64], low_ref[C_UR, 0:32, 0:64], ring_x[...].reshape(64, NZ)
-    )
-    ring_y[0] = times_const(column[0:16], high_ref[C_BD0], low_ref[C_BD0]) + times_const(
-        column[16:32], high_ref[C_BD1], low_ref[C_BD1]
-    )
-    round5 = []
-    for step in range(1, N_GY):
-        round5.append(send(34 + step, ring_y.at[0], ring_y.at[N_GY - step], 0, step))
-
     halo[2] = ring_x[0:3]
     for copy in round4:
         copy.wait_recv()
@@ -557,14 +579,16 @@
     table_copy.wait()
     for copy in round5:
         copy.wait_recv()
-    coarse = []
-    for row in range(9):
-        kind, shift = row % 4, row // 4
-
-        def add_slot(slot, total, kind=kind, shift=shift):
-            return total + table[kind, slot + 2 - shift] * ring_y[slot]
-
-        coarse.append(lax.fori_loop(0, N_GY, add_slot, jnp.zeros((16, NZ), F32), unroll=4))
+
+    def add_slot(slot, totals):
+        values = ring_y[slot]
+        return tuple(
+            total + table[row % 4, slot + 2 - row // 4] * values for row, total in enumerate(totals)
+        )
+
+    coarse = lax.fori_loop(
+        0, N_GY, add_slot, tuple(jnp.zeros((16, NZ), F32) for _ in range(9)), unroll=4
+    )
     coarse = jnp.concatenate(coarse, axis=0)
     half0 = times_const(coarse, high_ref[C_NZ0], low_ref[C_NZ0])
     half1 = times_const(coarse, high_ref[C_NZ1], low_ref[C_NZ1])
@@ -641,10 +665,15 @@
             pltpu.VMEM((2, 6, EY, NZ), F32),
             pltpu.VMEM((2, EX, 8, NZ), F32),
             pltpu.VMEM((4, 6, 8, NZ), F32),
+            pltpu.VMEM((2, 4, 16, NZ), F32),
+            pltpu.VMEM((2, 10, 8, NZ), F32),
+            pltpu.VMEM((4, 4, 8, NZ), F32),
+            pltpu.VMEM((10, 16, NZ), F32),
+            pltpu.VMEM((10, 8, NZ), F32),
             pltpu.VMEM((41, 40, NZ), F32),
             pltpu.VMEM((3, 41, EY, NZ), F32),
             pltpu.VMEM((EX, EY, NZ), F32),
-            pltpu.VMEM((37, 8, NZ), F32),
+            pltpu.VMEM((EX, 16, NZ), F32),
             pltpu.VMEM((26, 32, NZ), F32),
             pltpu.VMEM((20, 16, NZ), F32),
             pltpu.VMEM((8 * 24, NZ), F32),

time: 56.2 us -> 52.9 us (0.941)
  Pallas kernels: 55.4 us -> 52.1 us
    pallas_call x1, Pallas kernels: 46.6 us -> 43.3 us  [local(): pl.pallas_call(levels_kernel, out_shape=block, in_specs=in_vmem(11) + [pl...]
where the time goes in v2:
time: 52.9 us; the launch traced here: 52.8 us
  Pallas kernels  52.1 us (98%)
  between operations  0.64 us (1%)
    pallas_call x1, Pallas kernels, local(): pl.pallas_call(levels_kernel, out_shape=block, in_specs=in_vmem(11) + [pl...  43.3 us
    pallas_call x1, Pallas kernels, local(): pl.pallas_call(sample_kernel, out_shape=(jax.ShapeDtypeStruct((CX, CY, NZ...  8.82 us

profile of v2, /device:TPU:1, one launch (start us, length us, event | category | flops | bytes accessed | tf_op | source)
XLA Modules:
  0.0 52.8 jit_solution(5926944842183538561)
XLA Ops:
  0.6 43.3 %levels.1.field_ref = f32[35,24,128]{2,1,0:T(8,128)} custom-call(f32[1,16384]{1,0:T(1,128)} %bitcast.8, f32[3,1,16384]{2,1,0:T(1,128)} %bitcast.4, s32[2,16384]{1,0:T(2,128)} %bitcast.6, bf16[128,128]{1,0:T(8,128)(2,1)} %constant.22.clone.places_ref, bf16[128,128]{1,0:T(8,128)(2,1)} %constant.23.clone.forward_high_ref, ...), custom_call_target="tpu_custom_call" | custom-call | tf_op jit(solution)/shard_map/levels/pallas_call | solution.py:656
  43.9 8.8 %sample.1 = (f32[32,16,128]{2,1,0:T(8,128)}, f32[1,16384]{1,0:T(1,128)}) custom-call(f32[35,24,128]{2,1,0:T(8,128)} %levels.1.field_ref, f32[3,1,16384]{2,1,0:T(1,128)} %bitcast.5, s32[2,16384]{1,0:T(2,128)} %bitcast.7, bf16[128,128]{1,0:T(8,128)(2,1)} %constant.22.clone.places_ref, bf16[128,128]{1,0:T(8,128)(2,1)} %constant.25.clone.high_ref, ...), custom_call_target="tpu_custom_call" | custom-call | tf_op jit(solution)/shard_map/sample/pallas_call | solution.py:708

commit v3 on v2

--- a/solution.py
+++ b/solution.py
@@ -217,10 +217,17 @@
     return lanes, [w[0:1] for w in weights], table_y, tables_z
 
 
-def deposit_plane(plane, charge_ref, fraction_ref, cell_ref, places_ref, sums, index_y):
+def deposit_plane(
+    plane, charge_ref, fraction_ref, cell_ref, places_ref, sums, index_y, tables
+):
     lanes, along_x, table_y, (z_high, z_low) = plane_tables(
         plane, fraction_ref, cell_ref, places_ref, index_y
     )
+    keep_x, keep_y, keep_high, keep_low = tables
+    keep_x[plane] = jnp.concatenate(along_x, axis=0)
+    keep_y[plane] = table_y
+    keep_high[plane] = z_high
+    keep_low[plane] = z_low
     charge = charge_ref[:, lanes]
     spread = jnp.concatenate([table_y * (w * charge) for w in along_x], axis=0)
     spread_high, spread_low = split(spread)
@@ -233,38 +240,18 @@
         sums[plane + tap] = sums[plane + tap] + contrib[EY * tap : EY * (tap + 1)]
 
 
-def sample_kernel(
-    field_ref,
-    fraction_ref,
-    cell_ref,
-    places_ref,
-    high_ref,
-    low_ref,
-    grid_ref,
-    atom_ref,
-    window_ref,
-):
-    index_y = lax.axis_index("gy")
-    flat = field_ref[...].reshape(EX * EY, NZ)
-    window_ref[...] = times_const(flat, high_ref[...], low_ref[...]).reshape(EX, EY, NZ)
-    grid_ref[...] = window_ref[:CX, :CY, :]
-
-    def step(plane, carried):
-        lanes, along_x, table_y, (z_high, z_low) = plane_tables(
-            plane, fraction_ref, cell_ref, places_ref, index_y
-        )
-        window = window_ref[pl.ds(plane, 4)].reshape(4 * EY, NZ)
-        high, low = split(window)
-        projected = mm(
-            jnp.concatenate([high, low], axis=1), jnp.concatenate([z_high, z_high], axis=0)
-        ) + mm(high, z_low)
-        total = jnp.zeros((EY, PLANE), F32)
-        for tap in range(4):
-            total = total + along_x[tap] * projected[EY * tap : EY * (tap + 1)]
-        atom_ref[:, lanes] = jnp.sum(total * table_y, axis=0, keepdims=True)
-        return carried
-
-    lax.fori_loop(0, CX, step, 0, unroll=2)
+def sample_plane(plane, tables, window_ref, atom_ref):
+    keep_x, keep_y, keep_high, keep_low = tables
+    lanes = pl.ds(pl.multiple_of(plane * PLANE, PLANE), PLANE)
+    high, low = split(window_ref[pl.ds(plane, 4)].reshape(4 * EY, NZ))
+    z_high, z_low = keep_high[plane], keep_low[plane]
+    projected = mm(
+        jnp.concatenate([high, low], axis=1), jnp.concatenate([z_high, z_high], axis=0)
+    ) + mm(high, z_low)
+    total = jnp.zeros((EY, PLANE), F32)
+    for tap in range(4):
+        total = total + keep_x[plane, tap : tap + 1, :] * projected[EY * tap : EY * (tap + 1)]
+    atom_ref[:, lanes] = jnp.sum(total * keep_y[plane], axis=0, keepdims=True)
 
 
 NEIGHBOURS = ((1, 0), (-1, 0), (0, 1), (0, -1), (1, 1), (1, -1), (-1, 1), (-1, -1))
@@ -276,6 +263,22 @@
     if row % 2 == 0:
         return get(middle)
     return 0.5625 * (get(middle) + get(middle + 1)) - 0.0625 * (get(middle - 1) + get(middle + 2))
+
+
+N_IN = 14
+N_FIRST = 6
+
+
+def levels_entry(*refs):
+    sources, outputs = refs[:N_IN], refs[N_IN : N_IN + 2]
+    inputs, sems, rest = refs[N_IN + 2 : 2 * N_IN + 2], refs[2 * N_IN + 2], refs[2 * N_IN + 3 :]
+    copies = [
+        pltpu.make_async_copy(source, target, sems.at[number])
+        for number, (source, target) in enumerate(zip(sources, inputs))
+    ]
+    for copy in copies:
+        copy.start()
+    levels_kernel(*inputs, *outputs, *rest, copies[:N_FIRST], copies[N_FIRST:])
 
 
 def levels_kernel(
@@ -285,13 +288,21 @@
     places_ref,
     forward_high_ref,
     forward_low_ref,
+    inverse_high_ref,
+    inverse_low_ref,
     k1_ref,
     k2_ref,
     k3_ref,
     high_ref,
     low_ref,
-    table_hbm,
-    out_ref,
+    table,
+    grid_ref,
+    atom_ref,
+    keep_x,
+    keep_y,
+    keep_high,
+    keep_low,
+    window,
     sums,
     own,
     edge,
@@ -317,22 +328,20 @@
     field3,
     up3,
     up2,
-    table,
-    table_sem,
     send_sems,
     recv_sems,
+    first_copies,
+    later_copies,
 ):
     index_x = lax.axis_index("gx")
     index_y = lax.axis_index("gy")
+    tables = (keep_x, keep_y, keep_high, keep_low)
 
     def device(step_x, step_y):
         return (
             lax.rem(index_x + (step_x + N_GX), N_GX),
             lax.rem(index_y + (step_y + N_GY), N_GY),
         )
-
-    table_copy = pltpu.make_async_copy(table_hbm, table, table_sem)
-    table_copy.start()
 
     barrier = pltpu.get_barrier_semaphore()
     peers = [(x, 0) for x in range(1, N_GX)] + [(0, y) for y in range(1, N_GY)]
@@ -365,10 +374,13 @@
 
     lax.fori_loop(0, 41, clear, 0)
 
+    for copy in first_copies:
+        copy.wait()
+
     def deposit(first, last, row, count, send_finished):
         def step(plane, carried):
             deposit_plane(
-                plane, charge_ref, fraction_ref, cell_ref, places_ref, sums, index_y
+                plane, charge_ref, fraction_ref, cell_ref, places_ref, sums, index_y, tables
             )
             return carried
 
@@ -416,6 +428,9 @@
     deposit(6, 14, 6, 8, lambda: send_edges(10, 6, 8))
     deposit(14, 22, 14, 8, lambda: send_edges(12, 14, 8))
     deposit(22, 26, 22, 7, lambda: send_edges(14, 22, 7))
+
+    for copy in later_copies:
+        copy.wait()
 
     rows = []
     for m in range(-1, 19):
@@ -576,7 +591,6 @@
 
     lax.fori_loop(0, 9, stencil3, 0)
 
-    table_copy.wait()
     for copy in round5:
         copy.wait_recv()
 
@@ -626,17 +640,47 @@
 
     def widen_x(m, carried):
         values = [up2[m + n] for n in range(4)]
-        out_ref[2 * m] = smooth1[2 * m] + values[1]
-        out_ref[2 * m + 1] = smooth1[2 * m + 1] + (
+        sums[2 * m] = smooth1[2 * m] + values[1]
+        sums[2 * m + 1] = smooth1[2 * m + 1] + (
             0.5625 * (values[1] + values[2]) - 0.0625 * (values[0] + values[3])
         )
         return carried
 
     lax.fori_loop(0, 17, widen_x, 0)
-    out_ref[34] = smooth1[34] + up2[18]
+    sums[34] = smooth1[34] + up2[18]
+
+    flat = sums[...].reshape(EX * EY, NZ)
+    value = times_const(flat, inverse_high_ref[...], inverse_low_ref[...])
+    window[...] = value.reshape(EX, EY, NZ)
+    grid_ref[...] = window[:CX, :CY, :]
+
+    def sample(plane, carried):
+        sample_plane(plane, tables, window, atom_ref)
+        return carried
+
+    lax.fori_loop(0, CX, sample, 0, unroll=2)
 
     for copy in started:
         copy.wait_send()
+
+
+def finish_kernel(grid_in, atom_in, grid_out, atom_out, grid, atom, sems):
+    pairs = ((grid_in, grid, grid_out), (atom_in, atom, atom_out))
+    loads = [
+        pltpu.make_async_copy(source, middle, sems.at[number])
+        for number, (source, middle, target) in enumerate(pairs)
+    ]
+    stores = [
+        pltpu.make_async_copy(middle, target, sems.at[2 + number])
+        for number, (source, middle, target) in enumerate(pairs)
+    ]
+    for load in loads:
+        load.start()
+    for load, store in zip(loads, stores):
+        load.wait()
+        store.start()
+    for store in stores:
+        store.wait()
 
 
 def in_vmem(count):
@@ -650,15 +694,37 @@
     places = jnp.asarray(np.tile(np.arange(NZ)[:, None], (1, 128)).astype(BF16))
     forward = [jnp.asarray(part) for part in split_pair(real_basis(NZ).T)]
     inverse = [jnp.asarray(part) for part in split_pair(real_basis(NZ))]
-    block = jax.ShapeDtypeStruct((EX, EY, NZ), F32)
-
     high, low = split_constants()
-    field = pl.pallas_call(
-        levels_kernel,
-        out_shape=block,
-        in_specs=in_vmem(11) + [pl.BlockSpec(memory_space=pl.ANY)],
-        out_specs=pl.BlockSpec(memory_space=pltpu.VMEM),
-        scratch_shapes=[
+    inputs = [
+        charge,
+        fraction,
+        cell,
+        places,
+        *forward,
+        *inverse,
+        jnp.asarray(stencil_table(1, 128)),
+        jnp.asarray(stencil_table(2, 64)),
+        jnp.asarray(stencil_table(3, 32)),
+        jnp.asarray(high),
+        jnp.asarray(low),
+        jnp.asarray(coarse_table()),
+    ]
+    potential, sampled = pl.pallas_call(
+        levels_entry,
+        out_shape=(
+            jax.ShapeDtypeStruct((CX, CY, NZ), F32),
+            jax.ShapeDtypeStruct((1, ATOMS_DEV), F32),
+        ),
+        in_specs=[pl.BlockSpec(memory_space=pltpu.HBM)] * N_IN,
+        out_specs=in_vmem(2),
+        scratch_shapes=[pltpu.VMEM(value.shape, value.dtype) for value in inputs]
+        + [
+            pltpu.SemaphoreType.DMA((N_IN,)),
+            pltpu.VMEM((CX, 4, PLANE), F32),
+            pltpu.VMEM((CX, EY, PLANE), F32),
+            pltpu.VMEM((CX, NZ, PLANE), BF16),
+            pltpu.VMEM((CX, NZ, PLANE), BF16),
+            pltpu.VMEM((EX, EY, NZ), F32),
             pltpu.VMEM((EX, EY, NZ), F32),
             pltpu.VMEM((EX, EY, NZ), F32),
             pltpu.VMEM((EX, 8, NZ), F32),
@@ -684,38 +750,27 @@
             pltpu.VMEM((9, 16, NZ), F32),
             pltpu.VMEM((12 * 16, NZ), F32),
             pltpu.VMEM((20, EY, NZ), F32),
-            pltpu.VMEM((4, 34, 16, NZ), F32),
-            pltpu.SemaphoreType.DMA,
             pltpu.SemaphoreType.DMA((N_SEMS,)),
             pltpu.SemaphoreType.DMA((N_SEMS,)),
         ],
         compiler_params=pltpu.CompilerParams(collective_id=0, has_side_effects=True),
         name="levels",
-    )(
-        charge,
-        fraction,
-        cell,
-        places,
-        *forward,
-        jnp.asarray(stencil_table(1, 128)),
-        jnp.asarray(stencil_table(2, 64)),
-        jnp.asarray(stencil_table(3, 32)),
-        jnp.asarray(high),
-        jnp.asarray(low),
-        jnp.asarray(coarse_table()),
-    )
-
+    )(*inputs)
     potential, sampled = pl.pallas_call(
-        sample_kernel,
+        finish_kernel,
         out_shape=(
             jax.ShapeDtypeStruct((CX, CY, NZ), F32),
             jax.ShapeDtypeStruct((1, ATOMS_DEV), F32),
         ),
-        in_specs=in_vmem(6),
-        out_specs=in_vmem(2),
-        scratch_shapes=[pltpu.VMEM((EX, EY, NZ), F32)],
-        name="sample",
-    )(field, fraction, cell, places, *inverse)
+        in_specs=[pl.BlockSpec(memory_space=pl.ANY)] * 2,
+        out_specs=[pl.BlockSpec(memory_space=pl.ANY)] * 2,
+        scratch_shapes=[
+            pltpu.VMEM((CX, CY, NZ), F32),
+            pltpu.VMEM((1, ATOMS_DEV), F32),
+            pltpu.SemaphoreType.DMA((4,)),
+        ],
+        name="finish",
+    )(potential, sampled)
     return potential, sampled.reshape(1, 1, ATOMS_DEV)
 
 

time: 52.9 us -> 50.3 us (0.951)
  Pallas kernels: 52.1 us -> 49.6 us
    pallas_call x2, Pallas kernels: 52.1 us -> 49.6 us  [the longest x1 47.9 us: local(): pl.pallas_call(levels_entry, out_shape=(jax.ShapeDtypeStruct((CX, CY, NZ)...]
where the time goes in v3:
time: 50.3 us; the launch traced here: 50.2 us
  Pallas kernels  49.6 us (99%)
  between operations  0.64 us (1%)
    pallas_call x1, Pallas kernels, local(): pl.pallas_call(levels_entry, out_shape=(jax.ShapeDtypeStruct((CX, CY, NZ)...  47.9 us
    pallas_call x1, Pallas kernels, local(): pl.pallas_call(finish_kernel, out_shape=(jax.ShapeDtypeStruct((CX, CY, NZ...  1.7 us

profile of v3, /device:TPU:1, one launch (start us, length us, event | category | flops | bytes accessed | tf_op | source)
XLA Modules:
  0.0 50.2 jit_solution(15898334402889256910)
XLA Ops:
  0.6 47.9 %levels.1 = (f32[32,16,128]{2,1,0:T(8,128)}, f32[1,16384]{1,0:T(1,128)}) custom-call(f32[1,16384]{1,0:T(1,128)} %bitcast.6, f32[3,1,16384]{2,1,0:T(1,128)} %bitcast.4, s32[2,16384]{1,0:T(2,128)} %bitcast.5, bf16[128,128]{1,0:T(8,128)(2,1)} %constant.22.clone.refs_3_, bf16[128,128]{1,0:T(8,128)(2,1)} %constant.23.clone.refs_4_, ...), custom_call_target="tpu_custom_call" | custom-call | tf_op jit(solution)/shard_map/levels/pallas_call | solution.py:712
  48.5 1.7 %finish.1 = (f32[32,16,128]{2,1,0:T(8,128)}, f32[1,16384]{1,0:T(1,128)}) custom-call(f32[32,16,128]{2,1,0:T(8,128)} %get-tuple-element.6.grid_in, f32[1,16384]{1,0:T(1,128)} %get-tuple-element.7.atom_in), custom_call_target="tpu_custom_call" | custom-call | tf_op jit(solution)/shard_map/finish/pallas_call | solution.py:759

commit v4 on v3

--- a/solution.py
+++ b/solution.py
@@ -142,7 +142,7 @@
     folded = np.einsum("abcn,ny->abcy", folded, down_y)
     folded = folded.reshape(2, 16, 16, 4, 32, 4).transpose(3, 4, 1, 0, 5, 2)
     folded = folded.reshape(4, 32, 16, 128)
-    extended = folded[:, (np.arange(34) - 2) % 32]
+    extended = folded[:, (np.arange(35) - 3) % 32]
     return extended.astype(np.float32)
 
 
@@ -255,7 +255,9 @@
 
 
 NEIGHBOURS = ((1, 0), (-1, 0), (0, 1), (0, -1), (1, 1), (1, -1), (-1, 1), (-1, -1))
-N_SEMS = 16 + 8 + 7 + 4 + 31
+N_SEMS = 16 + 8 + 7 + 4 + 15 + 16
+HALF_GY = N_GY // 2
+FAR_FIRST = sorted(range(1, HALF_GY), key=lambda k: -min(k, HALF_GY - k))
 
 
 def prolonged_rows(get, row):
@@ -335,6 +337,7 @@
 ):
     index_x = lax.axis_index("gx")
     index_y = lax.axis_index("gy")
+    core = lax.rem(index_y, 2)
     tables = (keep_x, keep_y, keep_high, keep_low)
 
     def device(step_x, step_y):
@@ -344,7 +347,8 @@
         )
 
     barrier = pltpu.get_barrier_semaphore()
-    peers = [(x, 0) for x in range(1, N_GX)] + [(0, y) for y in range(1, N_GY)]
+    peers = [(x, 0) for x in range(1, N_GX)]
+    peers += [(0, y) for y in range(2, N_GY, 2)] + [(0, 1), (0, N_GY - 1)]
     peers += [(x, y) for x, y in NEIGHBOURS if x and y]
     for step_x, step_y in peers:
         pl.semaphore_signal(
@@ -446,7 +450,8 @@
     edge2[...] = own2[:, 5:13, :]
 
     round2 = []
-    for number, (step_x, step_y) in enumerate(NEIGHBOURS):
+    for number in (4, 5, 6, 7, 0, 1, 2, 3):
+        step_x, step_y = NEIGHBOURS[number]
         rows = {0: pl.ds(0, 10), 1: pl.ds(6, 4), -1: pl.ds(0, 4)}[step_x]
         if step_y == 0:
             source, target = own2.at[rows], from_x2.at[number]
@@ -496,7 +501,7 @@
     ring_x[1] = tile
 
     round3 = []
-    for step in range(1, N_GX):
+    for step in (4, 5, 3, 6, 2, 7, 1):
         place = (N_GX - step + 1) % N_GX
         round3.append(send(23 + step, ring_x.at[1], ring_x.at[place], step, 0))
 
@@ -527,12 +532,19 @@
     column = const_times(
         high_ref[C_UR, 0:32, 0:64], low_ref[C_UR, 0:32, 0:64], ring_x[...].reshape(64, NZ)
     )
-    ring_y[0] = times_const(column[0:16], high_ref[C_BD0], low_ref[C_BD0]) + times_const(
+    ring_y[core] = times_const(column[0:16], high_ref[C_BD0], low_ref[C_BD0]) + times_const(
         column[16:32], high_ref[C_BD1], low_ref[C_BD1]
     )
-    round5 = []
-    for step in range(1, N_GY):
-        round5.append(send(34 + step, ring_y.at[0], ring_y.at[N_GY - step], 0, step))
+    round5 = {}
+    for step in FAR_FIRST:
+        place = 2 * (HALF_GY - step) + core
+        round5[step] = send(34 + step, ring_y.at[core], ring_y.at[place], 0, 2 * step)
+
+    def hand_on(place):
+        row = ring_y.at[2 * place + core]
+        return send(50 + place, row, row, 0, 1 - 2 * core)
+
+    handed = [hand_on(0)]
 
     for copy in round1:
         copy.wait_recv()
@@ -575,6 +587,10 @@
 
     lax.fori_loop(0, EX, stencil1, 0)
 
+    for step in reversed(FAR_FIRST):
+        round5[step].wait_recv()
+        handed.append(hand_on(HALF_GY - step))
+
     halo[2] = ring_x[0:3]
     for copy in round4:
         copy.wait_recv()
@@ -591,13 +607,14 @@
 
     lax.fori_loop(0, 9, stencil3, 0)
 
-    for copy in round5:
+    for copy in handed:
         copy.wait_recv()
 
     def add_slot(slot, totals):
         values = ring_y[slot]
         return tuple(
-            total + table[row % 4, slot + 2 - row // 4] * values for row, total in enumerate(totals)
+            total + table[row % 4, slot + (3 - row // 4) - core] * values
+            for row, total in enumerate(totals)
         )
 
     coarse = lax.fori_loop(

time: 50.3 us -> 48.9 us (0.972)
  Pallas kernels: 49.6 us -> 48.2 us
    pallas_call x1, Pallas kernels: 47.9 us -> 46.5 us  [local(): pl.pallas_call(levels_entry, out_shape=(jax.ShapeDtypeStruct((CX, CY, NZ)...]
where the time goes in v4:
time: 48.9 us; the launch traced here: 48.8 us
  Pallas kernels  48.2 us (99%)
  between operations  0.64 us (1%)
    pallas_call x1, Pallas kernels, local(): pl.pallas_call(levels_entry, out_shape=(jax.ShapeDtypeStruct((CX, CY, NZ)...  46.5 us
    pallas_call x1, Pallas kernels, local(): pl.pallas_call(finish_kernel, out_shape=(jax.ShapeDtypeStruct((CX, CY, NZ...  1.7 us

profile of v4, /device:TPU:1, one launch (start us, length us, event | category | flops | bytes accessed | tf_op | source)
XLA Modules:
  0.0 48.8 jit_solution(14323182416091814183)
XLA Ops:
  0.6 46.5 %levels.1 = (f32[32,16,128]{2,1,0:T(8,128)}, f32[1,16384]{1,0:T(1,128)}) custom-call(f32[1,16384]{1,0:T(1,128)} %bitcast.6, f32[3,1,16384]{2,1,0:T(1,128)} %bitcast.4, s32[2,16384]{1,0:T(2,128)} %bitcast.5, bf16[128,128]{1,0:T(8,128)(2,1)} %constant.22.clone.refs_3_, bf16[128,128]{1,0:T(8,128)(2,1)} %constant.23.clone.refs_4_, ...), custom_call_target="tpu_custom_call" | custom-call | tf_op jit(solution)/shard_map/levels/pallas_call | solution.py:729
  47.1 1.7 %finish.1 = (f32[32,16,128]{2,1,0:T(8,128)}, f32[1,16384]{1,0:T(1,128)}) custom-call(f32[32,16,128]{2,1,0:T(8,128)} %get-tuple-element.6.grid_in, f32[1,16384]{1,0:T(1,128)} %get-tuple-element.7.atom_in), custom_call_target="tpu_custom_call" | custom-call | tf_op jit(solution)/shard_map/finish/pallas_call | solution.py:776

commit v5 on v4

--- a/solution.py
+++ b/solution.py
@@ -181,47 +181,72 @@
     )
 
 
-def tap_table(distance, weights):
-    result = jnp.zeros(distance.shape, F32)
-    for tap in range(4):
-        result = jnp.where(distance == tap, weights[tap], result)
-    return result
-
-
-def rows_of(row):
-    packed = jnp.broadcast_to(row, (16, row.shape[1])).astype(BF16)
-    return jnp.concatenate([packed] * (NZ // 16), axis=0)
-
-
-def depth_tables(places_ref, base, weights):
-    places = jnp.concatenate([places_ref[...]] * (base.shape[1] // 128), axis=1)
-    high = low = jnp.zeros(places.shape, BF16)
-    for tap in range(4):
-        target = ((base + tap) & (NZ - 1)).astype(F32)
-        here = places == rows_of(target)
-        weight_high = weights[tap].astype(BF16).astype(F32)
-        high = jnp.where(here, rows_of(weight_high), high)
-        low = jnp.where(here, rows_of(weights[tap] - weight_high), low)
-    return high, low
-
-
-def plane_tables(plane, fraction_ref, cell_ref, places_ref, index_y):
+BY_ROW = lax.GatherDimensionNumbers(
+    offset_dims=(),
+    collapsed_slice_dims=(0,),
+    start_index_map=(0,),
+    operand_batching_dims=(1,),
+    start_indices_batching_dims=(1,),
+)
+
+
+def picked(table, index):
+    return jnp.concatenate(
+        [
+            lax.gather(
+                table[:, lane : lane + 128],
+                index[:, lane : lane + 128, None],
+                BY_ROW,
+                slice_sizes=(1, 1),
+                mode=lax.GatherScatterMode.PROMISE_IN_BOUNDS,
+            )
+            for lane in range(0, table.shape[1], 128)
+        ],
+        axis=1,
+    )
+
+
+def eight_rows(rows):
+    return jnp.concatenate(rows + [jnp.zeros((4, rows[0].shape[1]), F32)], axis=0)
+
+
+def index_rows(base, first, period):
+    places = lax.broadcasted_iota(jnp.int32, (8, base.shape[1]), 0) + first
+    return jnp.minimum((places - base) & (period - 1), 7)
+
+
+def depth_tables(base, weights):
+    rounded = [w.astype(BF16).astype(F32) for w in weights]
+    high_rows = eight_rows(rounded)
+    low_rows = eight_rows([w - r for w, r in zip(weights, rounded)])
+    highs, lows = [], []
+    for first in range(0, NZ, 16):
+        indices = [index_rows(base, first + part, NZ) for part in (0, 8)]
+        for rows, result in ((high_rows, highs), (low_rows, lows)):
+            pair = jnp.concatenate([picked(rows, index) for index in indices], axis=0)
+            result.append(pair.astype(BF16))
+    return jnp.concatenate(highs, axis=0), jnp.concatenate(lows, axis=0)
+
+
+def plane_tables(plane, fraction_ref, cell_ref, index_y):
     lanes = pl.ds(pl.multiple_of(plane * PLANE, PLANE), PLANE)
     fraction = jnp.concatenate([fraction_ref[k, :, lanes] for k in range(3)], axis=0)
     weights = spline_weights(fraction)
     cells = cell_ref[:, lanes]
     base_y = (cells[0:1] - (index_y * CY + 1)) & (CY * N_GY - 1)
-    places_y = lax.broadcasted_iota(jnp.int32, (EY, PLANE), 0)
-    table_y = tap_table(places_y - base_y, [w[1:2] for w in weights])
-    tables_z = depth_tables(places_ref, cells[1:2] - 1, [w[2:3] for w in weights])
+    rows_y = eight_rows([w[1:2] for w in weights])
+    table_y = jnp.concatenate(
+        [picked(rows_y, index_rows(base_y, first, 32)) for first in range(0, EY, 8)], axis=0
+    )
+    tables_z = depth_tables(cells[1:2] - 1, [w[2:3] for w in weights])
     return lanes, [w[0:1] for w in weights], table_y, tables_z
 
 
 def deposit_plane(
-    plane, charge_ref, fraction_ref, cell_ref, places_ref, sums, index_y, tables
+    plane, charge_ref, fraction_ref, cell_ref, sums, index_y, tables
 ):
     lanes, along_x, table_y, (z_high, z_low) = plane_tables(
-        plane, fraction_ref, cell_ref, places_ref, index_y
+        plane, fraction_ref, cell_ref, index_y
     )
     keep_x, keep_y, keep_high, keep_low = tables
     keep_x[plane] = jnp.concatenate(along_x, axis=0)
@@ -267,8 +292,8 @@
     return 0.5625 * (get(middle) + get(middle + 1)) - 0.0625 * (get(middle - 1) + get(middle + 2))
 
 
-N_IN = 14
-N_FIRST = 6
+N_IN = 13
+N_FIRST = 5
 
 
 def levels_entry(*refs):
@@ -287,7 +312,6 @@
     charge_ref,
     fraction_ref,
     cell_ref,
-    places_ref,
     forward_high_ref,
     forward_low_ref,
     inverse_high_ref,
@@ -384,7 +408,7 @@
     def deposit(first, last, row, count, send_finished):
         def step(plane, carried):
             deposit_plane(
-                plane, charge_ref, fraction_ref, cell_ref, places_ref, sums, index_y, tables
+                plane, charge_ref, fraction_ref, cell_ref, sums, index_y, tables
             )
             return carried
 
@@ -708,7 +732,6 @@
     charge = charges.reshape(1, ATOMS_DEV)
     fraction = fractions.reshape(3, 1, ATOMS_DEV)
     cell = cells.reshape(2, ATOMS_DEV)
-    places = jnp.asarray(np.tile(np.arange(NZ)[:, None], (1, 128)).astype(BF16))
     forward = [jnp.asarray(part) for part in split_pair(real_basis(NZ).T)]
     inverse = [jnp.asarray(part) for part in split_pair(real_basis(NZ))]
     high, low = split_constants()
@@ -716,7 +739,6 @@
         charge,
         fraction,
         cell,
-        places,
         *forward,
         *inverse,
         jnp.asarray(stencil_table(1, 128)),

time: 48.9 us -> 48.4 us (0.990)
  Pallas kernels: 48.2 us -> 47.7 us
where the time goes in v5:
time: 48.4 us; the launch traced here: 48.3 us
  Pallas kernels  47.7 us (99%)
  between operations  0.64 us (1%)
    pallas_call x1, Pallas kernels, local(): pl.pallas_call(levels_entry, out_shape=(jax.ShapeDtypeStruct((CX, CY, NZ)...  46 us
    pallas_call x1, Pallas kernels, local(): pl.pallas_call(finish_kernel, out_shape=(jax.ShapeDtypeStruct((CX, CY, NZ...  1.7 us

profile of v5, /device:TPU:1, one launch (start us, length us, event | category | flops | bytes accessed | tf_op | source)
XLA Modules:
  0.0 48.3 jit_solution(13345303743532543117)
XLA Ops:
  0.6 46.0 %levels.1 = (f32[32,16,128]{2,1,0:T(8,128)}, f32[1,16384]{1,0:T(1,128)}) custom-call(f32[1,16384]{1,0:T(1,128)} %bitcast.6, f32[3,1,16384]{2,1,0:T(1,128)} %bitcast.4, s32[2,16384]{1,0:T(2,128)} %bitcast.5, bf16[128,128]{1,0:T(8,128)(2,1)} %constant.20.clone.refs_3_, bf16[128,128]{1,0:T(8,128)(2,1)} %constant.21.clone.refs_4_, ...), custom_call_target="tpu_custom_call" | custom-call | tf_op jit(solution)/shard_map/levels/pallas_call | solution.py:751
  46.6 1.7 %finish.1 = (f32[32,16,128]{2,1,0:T(8,128)}, f32[1,16384]{1,0:T(1,128)}) custom-call(f32[32,16,128]{2,1,0:T(8,128)} %get-tuple-element.6.grid_in, f32[1,16384]{1,0:T(1,128)} %get-tuple-element.7.atom_in), custom_call_target="tpu_custom_call" | custom-call | tf_op jit(solution)/shard_map/finish/pallas_call | solution.py:798

commit v6 on v5

--- a/solution.py
+++ b/solution.py
@@ -455,7 +455,7 @@
     deposit(0, 6, 0, 6, send_low)
     deposit(6, 14, 6, 8, lambda: send_edges(10, 6, 8))
     deposit(14, 22, 14, 8, lambda: send_edges(12, 14, 8))
-    deposit(22, 26, 22, 7, lambda: send_edges(14, 22, 7))
+    deposit(22, 26, 22, 7, lambda: None)
 
     for copy in later_copies:
         copy.wait()
@@ -486,6 +486,7 @@
             source = edge2.at[rows] if step_y == 1 else own2.at[rows, 0:8, :]
             target = from_corner2.at[number - 4]
         round2.append(send(16 + number, source, target, step_x, step_y))
+    send_edges(14, 22, 7)
 
     q2[...] = jnp.zeros_like(q2)
     q3[:, 24:32, :] = jnp.zeros((15, 8, NZ), F32)
@@ -550,9 +551,6 @@
     for copy in round3:
         copy.wait_recv()
 
-    round4 = []
-    for number, step in enumerate((1, -1, 2, -2)):
-        round4.append(send(31 + number, ring_x.at[0:3], halo.at[2 - step], 0, step))
     column = const_times(
         high_ref[C_UR, 0:32, 0:64], low_ref[C_UR, 0:32, 0:64], ring_x[...].reshape(64, NZ)
     )
@@ -569,6 +567,9 @@
         return send(50 + place, row, row, 0, 1 - 2 * core)
 
     handed = [hand_on(0)]
+    round4 = []
+    for number, step in enumerate((1, -1, 2, -2)):
+        round4.append(send(31 + number, ring_x.at[0:3], halo.at[2 - step], 0, step))
 
     for copy in round1:
         copy.wait_recv()

time: 48.4 us -> 47.9 us (0.990)
  Pallas kernels: 47.7 us -> 47.1 us
    pallas_call x1, Pallas kernels: 46 us -> 45.4 us  [local(): pl.pallas_call(levels_entry, out_shape=(jax.ShapeDtypeStruct((CX, CY, NZ)...]
where the time goes in v6:
time: 47.9 us; the launch traced here: 47.7 us
  Pallas kernels  47.1 us (98%)
  between operations  0.64 us (1%)
    pallas_call x1, Pallas kernels, local(): pl.pallas_call(levels_entry, out_shape=(jax.ShapeDtypeStruct((CX, CY, NZ)...  45.4 us
    pallas_call x1, Pallas kernels, local(): pl.pallas_call(finish_kernel, out_shape=(jax.ShapeDtypeStruct((CX, CY, NZ...  1.7 us

profile of v6, /device:TPU:1, one launch (start us, length us, event | category | flops | bytes accessed | tf_op | source)
XLA Modules:
  0.0 47.7 jit_solution(13318769157478688420)
XLA Ops:
  0.6 45.4 %levels.1 = (f32[32,16,128]{2,1,0:T(8,128)}, f32[1,16384]{1,0:T(1,128)}) custom-call(f32[1,16384]{1,0:T(1,128)} %bitcast.6, f32[3,1,16384]{2,1,0:T(1,128)} %bitcast.4, s32[2,16384]{1,0:T(2,128)} %bitcast.5, bf16[128,128]{1,0:T(8,128)(2,1)} %constant.20.clone.refs_3_, bf16[128,128]{1,0:T(8,128)(2,1)} %constant.21.clone.refs_4_, ...), custom_call_target="tpu_custom_call" | custom-call | tf_op jit(solution)/shard_map/levels/pallas_call | solution.py:752
  46.0 1.7 %finish.1 = (f32[32,16,128]{2,1,0:T(8,128)}, f32[1,16384]{1,0:T(1,128)}) custom-call(f32[32,16,128]{2,1,0:T(8,128)} %get-tuple-element.6.grid_in, f32[1,16384]{1,0:T(1,128)} %get-tuple-element.7.atom_in), custom_call_target="tpu_custom_call" | custom-call | tf_op jit(solution)/shard_map/finish/pallas_call | solution.py:799

commit v7 on v6

--- a/solution.py
+++ b/solution.py
@@ -454,7 +454,7 @@
     deposit(26, 32, 29, 6, send_high)
     deposit(0, 6, 0, 6, send_low)
     deposit(6, 14, 6, 8, lambda: send_edges(10, 6, 8))
-    deposit(14, 22, 14, 8, lambda: send_edges(12, 14, 8))
+    deposit(14, 22, 14, 8, lambda: None)
     deposit(22, 26, 22, 7, lambda: None)
 
     for copy in later_copies:
@@ -486,6 +486,7 @@
             source = edge2.at[rows] if step_y == 1 else own2.at[rows, 0:8, :]
             target = from_corner2.at[number - 4]
         round2.append(send(16 + number, source, target, step_x, step_y))
+    send_edges(12, 14, 8)
     send_edges(14, 22, 7)
 
     q2[...] = jnp.zeros_like(q2)
@@ -700,7 +701,7 @@
         sample_plane(plane, tables, window, atom_ref)
         return carried
 
-    lax.fori_loop(0, CX, sample, 0, unroll=2)
+    lax.fori_loop(0, CX, sample, 0, unroll=4)
 
     for copy in started:
         copy.wait_send()

time: 47.9 us -> 47.4 us (0.990)
  no operation moved by 1% of the time
where the time goes in v7:
time: 47.4 us; the launch traced here: 47.3 us
  Pallas kernels  46.7 us (99%)
  between operations  0.64 us (1%)
    pallas_call x1, Pallas kernels, local(): pl.pallas_call(levels_entry, out_shape=(jax.ShapeDtypeStruct((CX, CY, NZ)...  45 us
    pallas_call x1, Pallas kernels, local(): pl.pallas_call(finish_kernel, out_shape=(jax.ShapeDtypeStruct((CX, CY, NZ...  1.7 us

profile of v7, /device:TPU:1, one launch (start us, length us, event | category | flops | bytes accessed | tf_op | source)
XLA Modules:
  0.0 47.3 jit_solution(2324708418345506456)
XLA Ops:
  0.6 45.0 %levels.1 = (f32[32,16,128]{2,1,0:T(8,128)}, f32[1,16384]{1,0:T(1,128)}) custom-call(f32[1,16384]{1,0:T(1,128)} %bitcast.6, f32[3,1,16384]{2,1,0:T(1,128)} %bitcast.4, s32[2,16384]{1,0:T(2,128)} %bitcast.5, bf16[128,128]{1,0:T(8,128)(2,1)} %constant.20.clone.refs_3_, bf16[128,128]{1,0:T(8,128)(2,1)} %constant.21.clone.refs_4_, ...), custom_call_target="tpu_custom_call" | custom-call | tf_op jit(solution)/shard_map/levels/pallas_call | solution.py:753
  45.6 1.7 %finish.1 = (f32[32,16,128]{2,1,0:T(8,128)}, f32[1,16384]{1,0:T(1,128)}) custom-call(f32[32,16,128]{2,1,0:T(8,128)} %get-tuple-element.6.grid_in, f32[1,16384]{1,0:T(1,128)} %get-tuple-element.7.atom_in), custom_call_target="tpu_custom_call" | custom-call | tf_op jit(solution)/shard_map/finish/pallas_call | solution.py:800
